TPU v7x, 32 devices: a whole 2x2x4 slice. The times are simulated.
32 devices in a mesh: row: 8 (over y, x, core), col: 4 (over z).
Axes of the slice: x: 2, y: 2, z: 4, core: 2. Of those that a mesh axis runs over, the one named last changes fastest.
Arguments:
- ctrl_start: float32 [16384, 512], P(('row', 'col')), may hold values from -6 to 6
- obsv_start: float32 [16384, 512], P(('row', 'col')), may hold values from -6 to 6
- band_tiles: float32 [16384, 384], P(('row', 'col')), may hold values from -0.15625 to 0.15625
- band_offsets: int32 [128, 3], P(('row', 'col')), may hold values from -2 to 2, as said below
Outputs:
- cross_product: float32 [2048, 2048], P('row', 'col')
Inputs may be any that keep to these rules, and one draw needn't show every extreme that they name: `band_offsets`: the 3 offsets of a tile row are distinct.
All inputs are finite; a program needn't handle non-finite values.
Results may differ from a plain program's by a relative error of at most 0.0003.
Values sent between devices are 32-bit elements; how exact they have to be, the bound alone decides.
No kernel may reach another device: no remote copies, remote signals or barrier semaphores. Data moves between devices by JAX's collectives and lax.ppermute only.
A program may use at most 128 MiB of HBM per device.

v0:
```python
import functools
import math

import jax
import jax.numpy as jnp
from jax import lax
from jax.experimental import pallas as pl
from jax.experimental.pallas import tpu as pltpu
from jax.sharding import PartitionSpec as P

TILE = 128
HALO = 2
BAND = 3
ORDERS = 4
AXES = ("row", "col")
VMEM = pltpu.VMEM
GRANT = 16 * 2**20
ROW_GROUPS = ((0,), (1, 2), (3, 4), (5,), (6,))
COL_GROUPS = ((0, 1, 2), (3, 4), (5,), (6,))


def call(kernel, outs, ins, scratch=(), flops=0, bytes_=0, scalars=0):
    specs = [pl.BlockSpec(memory_space=pltpu.SMEM)] * scalars
    specs += [pl.BlockSpec(memory_space=VMEM)] * (len(ins) - scalars)
    return pl.pallas_call(
        kernel,
        out_shape=outs,
        in_specs=specs,
        out_specs=jax.tree.map(lambda _: pl.BlockSpec(memory_space=VMEM), outs),
        scratch_shapes=list(scratch),
        cost_estimate=pl.CostEstimate(flops=flops, bytes_accessed=bytes_, transcendentals=0),
        compiler_params=pltpu.CompilerParams(vmem_limit_bytes=GRANT),
    )(*ins)


def split(value):
    high = value.astype(jnp.bfloat16)
    return high, (value - high.astype(jnp.float32)).astype(jnp.bfloat16)


def dot(a, b):
    return jnp.dot(a, b, preferred_element_type=jnp.float32)


def forward_kernel(offs, pos, outer, inner, from_outer, from_inner, tiles, outer_out, inner_out, high, low):
    margin = HALO * TILE
    odd = pos[4]
    placed = ((from_outer, 3 * odd), (outer, 1 + odd), (inner, 2 - odd), (from_inner, 3 - 3 * odd))
    for ref, place in placed:
        here = pl.ds(pl.multiple_of(place * margin, margin), margin)
        high[here, :], low[here, :] = split(ref[...])
    for out, base in ((outer_out, HALO * odd), (inner_out, HALO * (1 - odd))):
        for i in range(HALO):
            index = base + i
            starts = [
                pl.multiple_of((index + HALO + offs[index, b]) * TILE, TILE) for b in range(BAND)
            ]
            stack_high = jnp.concatenate([high[pl.ds(s, TILE), :] for s in starts], 0)
            stack_low = jnp.concatenate([low[pl.ds(s, TILE), :] for s in starts], 0)
            tile_high, tile_low = split(tiles[pl.ds(pl.multiple_of(index * TILE, TILE), TILE), :])
            out[i * TILE : (i + 1) * TILE, :] = dot(tile_high, stack_high) + (
                dot(tile_high, stack_low) + dot(tile_low, stack_high)
            )


def forward(offs, pos, outer, inner, from_outer, from_inner, tiles):
    shape = jax.ShapeDtypeStruct(outer.shape, jnp.float32)
    rows, width = 2 * outer.shape[0], outer.shape[1]
    scratch = [VMEM((2 * rows, width), jnp.bfloat16)] * 2
    return call(
        forward_kernel, (shape, shape), (offs, pos, outer, inner, from_outer, from_inner, tiles),
        scratch, 6 * rows * BAND * TILE * width, 4 * (4 * rows * width), 2,
    )


def turn_kernel(parts, quarters, pos, *refs):
    *sources, high_out, low_out = refs
    turned = jnp.concatenate([ref[...].T for ref in sources], 1)
    high, low = split(turned)
    width = high.shape[0] // (parts * quarters)
    for d in range(parts):
        for e in range(quarters):
            for p in range(parts):
                for q in range(quarters):
                    @pl.when(jnp.logical_and((pos[0] + d) % parts == p, (pos[1] + e) % quarters == q))
                    def _(d=d, e=e, p=p, q=q):
                        here = (d * quarters + e) * width
                        there = (p * quarters + q) * width
                        high_out[here : here + width, :] = high[there : there + width]
                        low_out[here : here + width, :] = low[there : there + width]


def turn(parts, pos, sources):
    rows, width = sum(x.shape[0] for x in sources), sources[0].shape[1]
    half = jax.ShapeDtypeStruct((width, rows), jnp.bfloat16)
    return call(
        functools.partial(turn_kernel, parts, ORDERS), (half, half), (pos, *sources), (),
        width * width, 8 * width * rows, 1,
    )


def product_kernel(parts, high, low, *refs):
    sources, outs = refs[:-parts], refs[-parts:]
    right_high, right_low = split(jnp.concatenate([ref[...] for ref in sources], 0))
    rows = high.shape[0] // parts
    for d, out in enumerate(outs):
        here = pl.ds(d * rows, rows)
        a = high[here, :]
        out[...] = dot(a, right_high) + (dot(a, right_low) + dot(low[here, :], right_high))


def product(turned, sources, parts):
    high, low = turned
    rows, width = high.shape[0], sources[0].shape[1]
    shapes = tuple(jax.ShapeDtypeStruct((rows // parts, width), jnp.float32) for _ in range(parts))
    return call(
        functools.partial(product_kernel, parts), shapes, (high, low, *sources), (),
        6 * rows * width * high.shape[1], 4 * 4 * rows * width,
    )


def pick_kernel(count, pos, *refs):
    sources, outs = refs[: -count], refs[-count:]
    for d, out in enumerate(outs):
        power = (pos[1] + d) % count + pos[2]
        for k, ref in enumerate(sources):
            @pl.when(power == k)
            def _(out=out, ref=ref):
                out[...] = ref[...]


def place_kernel(scale, pos, *refs):
    *parts, out = refs
    count = len(parts)
    rows = parts[0].shape[0]
    for d, ref in enumerate(parts):
        at = (pos[1] + count - d) % count
        out[pl.ds(pl.multiple_of(at * rows, rows), rows), :] = ref[...] * scale


def local(rows_all, cols_all, ctrl, obsv, tiles, offs):
    total = rows_all * cols_all
    parts, splits = rows_all // ORDERS, cols_all // ORDERS
    r, c = lax.axis_index("row"), lax.axis_index("col")
    big_row, part, big_col, piece = r // parts, r % parts, c // splits, c % splits
    pos = jnp.stack([part, big_row, big_col, piece, r % 2]).astype(jnp.int32)
    devices = [(i, j) for i in range(rows_all) for j in range(cols_all)]

    def flat(i, j):
        return i * cols_all + j

    def permute(x, pairs):
        return lax.ppermute(x, AXES, pairs)

    def peers(move):
        return [(flat(i, j), flat(*move(i, j))) for i, j in devices]

    def seat(s):
        lane, q = divmod(s, 2 * cols_all)
        j = q // 2 if lane % 2 == 0 else cols_all - 1 - q // 2
        return flat(2 * lane + q % 2, j)

    seats = [seat(s) for s in range(total)]
    relay = [(s, seats[s]) for s in range(total)]
    inside = [(seats[s], seats[s ^ 1]) for s in range(total)]
    across = [(seats[s], seats[s + 1]) for s in range(1, total - 1, 2)]
    across += [(b, a) for a, b in across]

    margin = HALO * TILE
    width = ctrl.shape[1]
    quarter = width // (parts * ORDERS)

    def halves(x):
        first = (c % 2) * margin
        return (
            lax.dynamic_slice_in_dim(x, first, margin, 0),
            lax.dynamic_slice_in_dim(x, margin - first, margin, 0),
        )

    first, second = halves(ctrl)
    far_first, far_second = halves(obsv)
    moved_offs = permute(offs, relay)
    outer = permute(first, relay)
    inner = permute(second, relay)
    moved_tiles = permute(tiles, relay)
    far = (permute(far_first, relay), permute(far_second, relay))
    near_turned = turn(parts, pos, (obsv,))
    far_turned = turn(parts, pos, far)

    def over_parts(blocks):
        kept = blocks[0]
        for d in range(1, parts):
            move = peers(lambda i, j: ((i // parts) * parts + (i + d) % parts, j))
            kept = kept + permute(blocks[d], move)
        if splits == 1:
            return kept
        wide = kept.shape[1] // splits
        cut = [
            lax.dynamic_slice_in_dim(kept, ((piece + d) % splits) * wide, wide, 1)
            for d in range(splits)
        ]
        kept = cut[0]
        for d in range(1, splits):
            move = peers(lambda i, j: (i, (j // splits) * splits + (j + d) % splits))
            kept = kept + permute(cut[d], move)
        return kept

    def turned(i, e):
        return ((i // parts + e) % ORDERS) * parts + i % parts

    def over_rows(block):
        kept = block[:, :quarter]
        for e in range(1, ORDERS):
            sent = block[:, e * quarter : (e + 1) * quarter]
            kept = kept + permute(sent, peers(lambda i, j: (turned(i, e), j)))
        return kept

    def line(moves):
        return [
            (flat(i, a * splits + s), flat(i, b * splits + s))
            for a, b in moves for i in range(rows_all) for s in range(splits)
        ]

    def over_cols(own, powers):
        low_k, high_k = min(powers), max(powers)
        last = 2 * ORDERS - 2
        first = []
        if high_k >= 1:
            first.append((0, 1))
        if low_k < last:
            first.append((3, 2))
        second = []
        if high_k >= 2:
            second.append((1, 2))
        if low_k <= last - 2:
            second.append((2, 1))
        third = []
        if low_k <= ORDERS - 1:
            third.append((1, 0))
        if high_k >= ORDERS - 1:
            third.append((2, 3))
        both = own + permute(own, line(first))
        both = both + permute(both, line(second))
        ends = permute(both, line(third))
        if (3, 2) not in first:
            ends = ends + jnp.where(big_col == 3, own, 0.0)
        outer = jnp.logical_or(big_col == 0, big_col == 3)
        return jnp.where(outer, ends, both)

    def over_top(own):
        got = own
        for a in range(ORDERS - 1):
            got = got + permute(own, line([(a, ORDERS - 1)]))
        return got

    sums, rows_done, kept = {}, {}, {}

    def reduce_ready():
        for group in ROW_GROUPS:
            if all(k in sums for k in group) and group[0] not in rows_done:
                done = over_rows(jnp.stack([sums[k] for k in group]))
                for at, k in enumerate(group):
                    rows_done[k] = done[at : at + 1]
        for group in COL_GROUPS:
            if all(k in rows_done for k in group) and group[0] not in kept:
                own = jnp.concatenate([rows_done[k] for k in group], 0)
                done = over_top(own) if group == (2 * ORDERS - 2,) else over_cols(own, group)
                for at, k in enumerate(group):
                    kept[k] = done[at]

    sums[0] = over_parts(product(near_turned, (ctrl,), parts))
    reduce_ready()
    for k in range(1, 2 * ORDERS - 1):
        from_inner = permute(inner, inside)
        from_outer = permute(outer, across)
        outer, inner = forward(moved_offs, pos, outer, inner, from_outer, from_inner, moved_tiles)
        sums[k] = over_parts(product(far_turned, (outer, inner), parts))
        reduce_ready()

    shape = kept[0].shape
    block = jax.ShapeDtypeStruct(shape, jnp.float32)
    sent = call(
        functools.partial(pick_kernel, ORDERS), (block,) * ORDERS,
        (pos, *[kept[k] for k in range(2 * ORDERS - 1)]), (), shape[0] * shape[1], 44 * shape[0] * shape[1], 1,
    )
    got = [sent[0]] + [permute(sent[d], peers(lambda i, j: (turned(i, d), j))) for d in range(1, ORDERS)]
    out = jax.ShapeDtypeStruct((ORDERS * shape[0], shape[1]), jnp.float32)
    scale = 1.0 / math.sqrt(ctrl.shape[0] * total)
    return call(
        functools.partial(place_kernel, scale), out, (pos, *got), (),
        shape[0] * shape[1], 32 * shape[0] * shape[1], 1,
    )


def solution(mesh):
    rows_all, cols_all = mesh.shape["row"], mesh.shape["col"]

    def body(*args):
        return local(rows_all, cols_all, *args)

    return jax.shard_map(
        body,
        mesh=mesh,
        in_specs=(P(AXES, None),) * 4,
        out_specs=P("row", "col"),
        check_vma=False,
    )
```

profile of v0, /device:TPU:0, one launch (start us, length us, event | category | flops | bytes accessed | tf_op | source)
XLA Modules:
  0.0 215.6 jit_solution(17666507610941366269)
XLA Ops:
  0.0 1.4 constant_dynamic-slice_fusion
  2.8 1.8 collective-permute-start.11
  4.6 1.5 collective-permute-start.9
  6.1 31.2 %collective-permute-start.10 = (f32[256,512]{1,0:T(8,128)S(1)}, f32[256,512]{1,0:T(8,128)}, u32[]{:S(2)}, u32[]{:S(2)}) collective-permute-start(f32[256,512]{1,0:T(8,128)S(1)} %collective-permute-done.8.inner), channel_id=1, source_target_pairs={{0,4},{4,0},{1,5},{5,1},{2,6},{6,2},{3,7},{7,3},{11,15},{15,11},{1... | collective-permute-start | bytes 1572872 | tf_op jit(solution)/shard_map/ppermute | solution.py:153
  38.3 1.7 collective-permute-start.4
  40.7 1.7 collective-permute-start.5
  42.4 1.9 shard_map.46
  44.4 2.8 %shard_map.49 = (f32[256,512]{1,0:T(8,128)S(1)}, f32[256,512]{1,0:T(8,128)S(1)}) custom-call(s32[4,3]{1,0:T(4,128)S(1)} %collective-permute-done.6.offs, s32[5]{0:T(128)S(1)} %stack.44.pos, f32[256,512]{1,0:T(8,128)S(1)} %collective-permute-done.7.outer, f32[256,512]{1,0:T(8,128)S(1)} %collective-permute-done.8.inner, ...), custom_call_target="tpu_custom_call" | custom-call | flops 603979776 | bytes 4194304 | tf_op jit(solution)/shard_map/pallas_call | solution.py:25
  47.9 27.0 %collective-permute-start.14 = (f32[256,512]{1,0:T(8,128)S(1)}, f32[256,512]{1,0:T(8,128)S(1)}, u32[]{:S(2)}, u32[]{:S(2)}) collective-permute-start(f32[256,512]{1,0:T(8,128)S(1)} %get-tuple-element.46.refs_1_.inner), channel_id=1, source_target_pairs={{0,4},{4,0},{1,5},{5,1},{2,6},{6,2},{3,7},{7,3},{11,15},{15,11},{1... | collective-permute-start | bytes 1572872 | tf_op jit(solution)/shard_map/ppermute | solution.py:153
  75.9 1.9 shard_map.48
  79.4 2.1 shard_map.51
  82.1 6.7 %collective-permute-start.23 = (f32[256,512]{1,0:T(8,128)S(1)}, f32[256,512]{1,0:T(8,128)S(1)}, u32[]{:S(2)}, u32[]{:S(2)}) collective-permute-start(f32[256,512]{1,0:T(8,128)S(1)} %get-tuple-element.50.refs_1_.inner), channel_id=1, source_target_pairs={{0,4},{4,0},{1,5},{5,1},{2,6},{6,2},{3,7},{7,3},{11,15},{15,11},{1... | collective-permute-start | bytes 1572872 | tf_op jit(solution)/shard_map/ppermute | solution.py:153
  90.0 5.4 %collective-permute-start.3 = (f32[1,64,512]{2,1,0:T(8,128)S(1)}, f32[1,64,512]{2,1,0:T(8,128)S(1)}, u32[]{:S(2)}, u32[]{:S(2)}) collective-permute-start(f32[1,64,512]{2,1,0:T(8,128)S(1)} %get-tuple-element.90), channel_id=1, source_target_pairs={{0,24},{1,25},{2,26},{3,27},{4,28},{5,29},{6,30},{7,31},{8,0},{9,1... | collective-permute-start | bytes 393224 | tf_op jit(solution)/shard_map/ppermute | solution.py:153
  95.4 4.4 %collective-permute-start.2 = (f32[1,64,512]{2,1,0:T(8,128)S(1)}, f32[1,64,512]{2,1,0:T(8,128)S(1)}, u32[]{:S(2)}, u32[]{:S(2)}) collective-permute-start(f32[1,64,512]{2,1,0:T(8,128)S(1)} %get-tuple-element.91), channel_id=1, source_target_pairs={{0,16},{1,17},{2,18},{3,19},{4,20},{5,21},{6,22},{7,23},{8,24},{9,... | collective-permute-start | bytes 393224 | tf_op jit(solution)/shard_map/ppermute | solution.py:153
  99.8 2.2 %collective-permute-start.1 = (f32[1,64,512]{2,1,0:T(8,128)S(1)}, f32[1,64,512]{2,1,0:T(8,128)S(1)}, u32[]{:S(2)}, u32[]{:S(2)}) collective-permute-start(f32[1,64,512]{2,1,0:T(8,128)S(1)} %get-tuple-element.89), channel_id=1, source_target_pairs={{0,8},{1,9},{2,10},{3,11},{4,12},{5,13},{6,14},{7,15},{8,16},{9,17... | collective-permute-start | bytes 393224 | tf_op jit(solution)/shard_map/ppermute | solution.py:153
  102.1 2.0 shard_map.53
  105.1 3.6 %collective-permute-start.26 = (f32[256,512]{1,0:T(8,128)S(1)}, f32[256,512]{1,0:T(8,128)S(1)}, u32[]{:S(2)}, u32[]{:S(2)}) collective-permute-start(f32[256,512]{1,0:T(8,128)S(1)} %get-tuple-element.54.refs_1_.inner), channel_id=1, source_target_pairs={{0,4},{4,0},{1,5},{5,1},{2,6},{6,2},{3,7},{7,3},{11,15},{15,11},{1... | collective-permute-start | bytes 1572872 | tf_op jit(solution)/shard_map/ppermute | solution.py:153
  110.0 1.2 collective-permute-start.17
  111.2 1.4 collective-permute-start.16
  112.5 3.0 %collective-permute-start.24 = (f32[256,512]{1,0:T(8,128)S(1)}, f32[256,512]{1,0:T(8,128)S(1)}, u32[]{:S(2)}, u32[]{:S(2)}) collective-permute-start(f32[256,512]{1,0:T(8,128)S(1)} %get-tuple-element.56), channel_id=1, source_target_pairs={{0,4},{1,5},{2,6},{3,7},{4,0},{5,1},{6,2},{7,3},{8,12},{9,13},{10,... | collective-permute-start | bytes 1572872 | tf_op jit(solution)/shard_map/ppermute | solution.py:153
  115.6 2.1 shard_map.55
  119.2 4.8 %collective-permute-done.17 = f32[2,64,512]{2,1,0:T(8,128)S(1)} collective-permute-done((f32[2,64,512]{2,1,0:T(8,128)S(1)}, f32[2,64,512]{2,1,0:T(8,128)S(1)}, u32[]{:S(2)}, u32[]{:S(2)}) %collective-permute-start.17) | collective-permute-done | bytes 262176 | tf_op jit(solution)/shard_map/ppermute | solution.py:153
  124.0 3.6 %collective-permute-start.19 = (f32[3,64,512]{2,1,0:T(8,128)S(1)}, f32[3,64,512]{2,1,0:T(8,128)S(1)}, u32[]{:S(2)}, u32[]{:S(2)}) collective-permute-start(f32[3,64,512]{2,1,0:T(8,128)S(1)} %pad_maximum_fusion), channel_id=1, source_target_pairs={{0,1},{4,5},{8,9},{12,13},{16,17},{20,21},{24,25},{28,29},{3,2},{7... | collective-permute-start | bytes 1179656 | tf_op jit(solution)/shard_map/ppermute | solution.py:153
  129.4 1.9 collective-permute-start.30
  131.3 3.3 %collective-permute-start.29 = (f32[2,64,512]{2,1,0:T(8,128)S(1)}, f32[2,64,512]{2,1,0:T(8,128)S(1)}, u32[]{:S(2)}, u32[]{:S(2)}) collective-permute-start(f32[2,64,512]{2,1,0:T(8,128)S(1)} %get-tuple-element.75), channel_id=1, source_target_pairs={{0,16},{1,17},{2,18},{3,19},{4,20},{5,21},{6,22},{7,23},{8,24},{9,... | collective-permute-start | bytes 786440 | tf_op jit(solution)/shard_map/ppermute | solution.py:153
  134.5 8.5 %collective-permute-start.28 = (f32[2,64,512]{2,1,0:T(8,128)S(1)}, f32[2,64,512]{2,1,0:T(8,128)S(1)}, u32[]{:S(2)}, u32[]{:S(2)}) collective-permute-start(f32[2,64,512]{2,1,0:T(8,128)S(1)} %get-tuple-element.73), channel_id=1, source_target_pairs={{0,8},{1,9},{2,10},{3,11},{4,12},{5,13},{6,14},{7,15},{8,16},{9,17... | collective-permute-start | bytes 786440 | tf_op jit(solution)/shard_map/ppermute | solution.py:153
  143.0 2.0 shard_map.57
  145.1 1.8 shard_map.58
  147.7 1.4 collective-permute-start.20
  150.6 6.7 %collective-permute-start.31 = (f32[2,64,512]{2,1,0:T(8,128)}, f32[2,64,512]{2,1,0:T(8,128)}, u32[]{:S(2)}, u32[]{:S(2)}) collective-permute-start(f32[2,64,512]{2,1,0:T(8,128)} %fusion.4), channel_id=1, source_target_pairs={{0,1},{4,5},{8,9},{12,13},{16,17},{20,21},{24,25},{28,29},{3,2},{7... | collective-permute-start | bytes 786440 | tf_op jit(solution)/shard_map/ppermute | solution.py:153
  158.0 1.2 collective-permute-start.44
  159.2 1.2 add.128
  160.4 1.3 collective-permute-start.21
  161.7 1.9 collective-permute-done.31
  166.6 2.6 %collective-permute-start.38 = (f32[1,64,512]{2,1,0:T(8,128)S(1)}, f32[1,64,512]{2,1,0:T(8,128)S(1)}, u32[]{:S(2)}, u32[]{:S(2)}) collective-permute-start(f32[1,64,512]{2,1,0:T(8,128)S(1)} %get-tuple-element.88), channel_id=1, source_target_pairs={{0,16},{1,17},{2,18},{3,19},{4,20},{5,21},{6,22},{7,23},{8,24},{9,... | collective-permute-start | bytes 393224 | tf_op jit(solution)/shard_map/ppermute | solution.py:153
  169.2 2.1 shard_map.59
  172.4 3.6 %collective-permute-done.38 = f32[1,64,512]{2,1,0:T(8,128)S(1)} collective-permute-done((f32[1,64,512]{2,1,0:T(8,128)S(1)}, f32[1,64,512]{2,1,0:T(8,128)S(1)}, u32[]{:S(2)}, u32[]{:S(2)}) %collective-permute-start.38) | collective-permute-done | bytes 131104 | tf_op jit(solution)/shard_map/ppermute | solution.py:153
  176.0 6.1 %collective-permute-start.40 = (f32[1,64,512]{2,1,0:T(8,128)S(1)}, f32[1,64,512]{2,1,0:T(8,128)S(1)}, u32[]{:S(2)}, u32[]{:S(2)}) collective-permute-start(f32[1,64,512]{2,1,0:T(8,128)S(1)} %fusion.15), channel_id=1, source_target_pairs={{0,1},{4,5},{8,9},{12,13},{16,17},{20,21},{24,25},{28,29},{3,2},{7... | collective-permute-start | bytes 393224 | tf_op jit(solution)/shard_map/ppermute | solution.py:153
  182.2 2.4 %collective-permute-done.40 = f32[1,64,512]{2,1,0:T(8,128)S(1)} collective-permute-done((f32[1,64,512]{2,1,0:T(8,128)S(1)}, f32[1,64,512]{2,1,0:T(8,128)S(1)}, u32[]{:S(2)}, u32[]{:S(2)}) %collective-permute-start.40) | collective-permute-done | bytes 131104 | tf_op jit(solution)/shard_map/ppermute | solution.py:153
  185.4 1.3 collective-permute-start.33
  188.4 1.3 collective-permute-start.47
  190.6 5.9 %collective-permute-done.33 = f32[2,64,512]{2,1,0:T(8,128)S(1)} collective-permute-done((f32[2,64,512]{2,1,0:T(8,128)S(1)}, f32[2,64,512]{2,1,0:T(8,128)S(1)}, u32[]{:S(2)}, u32[]{:S(2)}) %collective-permute-start.33) | collective-permute-done | bytes 262176 | tf_op jit(solution)/shard_map/ppermute | solution.py:153
  197.9 5.7 %collective-permute-start.49 = (f32[1,64,512]{2,1,0:T(8,128)S(1)}, f32[1,64,512]{2,1,0:T(8,128)S(1)}, u32[]{:S(2)}, u32[]{:S(2)}) collective-permute-start(f32[1,64,512]{2,1,0:T(8,128)S(1)} %fusion.13), channel_id=1, source_target_pairs={{0,3},{4,7},{8,11},{12,15},{16,19},{20,23},{24,27},{28,31}} | collective-permute-start | bytes 393224 | tf_op jit(solution)/shard_map/ppermute | solution.py:153
  203.7 2.4 %collective-permute-done.49 = f32[1,64,512]{2,1,0:T(8,128)S(1)} collective-permute-done((f32[1,64,512]{2,1,0:T(8,128)S(1)}, f32[1,64,512]{2,1,0:T(8,128)S(1)}, u32[]{:S(2)}, u32[]{:S(2)}) %collective-permute-start.49) | collective-permute-done | bytes 131104 | tf_op jit(solution)/shard_map/ppermute | solution.py:153
  207.6 1.4 collective-permute-start.53
  209.0 2.3 %collective-permute-start.54 = (f32[64,512]{1,0:T(8,128)S(1)}, f32[64,512]{1,0:T(8,128)S(1)}, u32[]{:S(2)}, u32[]{:S(2)}) collective-permute-start(f32[64,512]{1,0:T(8,128)S(1)} %get-tuple-element.72), channel_id=1, source_target_pairs={{0,24},{1,25},{2,26},{3,27},{4,28},{5,29},{6,30},{7,31},{8,0},{9,1... | collective-permute-start | bytes 393224 | tf_op jit(solution)/shard_map/ppermute | solution.py:153
  211.3 1.6 collective-permute-done.52.refs_1_
  214.2 1.4 shard_map.62
  (126 shorter events, 28.4 us)
Async XLA Ops:
  2.8 41.6 %collective-permute-start.11 = (f32[512,384]{1,0:T(8,128)}, f32[512,384]{1,0:T(8,128)S(1)}, u32[]{:S(2)}, u32[]{:S(2)}) collective-permute-start(f32[512,384]{1,0:T(8,128)} %param.6), channel_id=1, source_target_pairs={{0,0},{1,4},{2,1},{3,5},{4,2},{5,6},{6,3},{7,7},{8,11},{9,15},{10,... | collective-permute-start | bytes 2359304 | tf_op jit(solution)/shard_map/ppermute | solution.py:153
  4.6 39.8 %collective-permute-start.9 = (f32[256,512]{1,0:T(8,128)S(1)}, f32[256,512]{1,0:T(8,128)}, u32[]{:S(2)}, u32[]{:S(2)}) collective-permute-start(f32[256,512]{1,0:T(8,128)S(1)} %collective-permute-done.7.outer), channel_id=1, source_target_pairs={{4,1},{5,2},{6,3},{7,11},{15,10},{14,9},{13,8},{12,16},{20,17},{21... | collective-permute-start | bytes 1572872 | tf_op jit(solution)/shard_map/ppermute | solution.py:153
  6.1 38.3 %collective-permute-start.10 = (f32[256,512]{1,0:T(8,128)S(1)}, f32[256,512]{1,0:T(8,128)}, u32[]{:S(2)}, u32[]{:S(2)}) collective-permute-start(f32[256,512]{1,0:T(8,128)S(1)} %collective-permute-done.8.inner), channel_id=1, source_target_pairs={{0,4},{4,0},{1,5},{5,1},{2,6},{6,2},{3,7},{7,3},{11,15},{15,11},{1... | collective-permute-start | bytes 1572872 | tf_op jit(solution)/shard_map/ppermute | solution.py:153
  38.3 37.6 %collective-permute-start.4 = (f32[256,512]{1,0:T(8,128)}, f32[256,512]{1,0:T(8,128)S(1)}, u32[]{:S(2)}, u32[]{:S(2)}) collective-permute-start(f32[256,512]{1,0:T(8,128)} %get-tuple-element.82), channel_id=1, source_target_pairs={{0,0},{1,4},{2,1},{3,5},{4,2},{5,6},{6,3},{7,7},{8,11},{9,15},{10,... | collective-permute-start | bytes 1572872 | tf_op jit(solution)/shard_map/ppermute | solution.py:153
  40.7 35.2 %collective-permute-start.5 = (f32[256,512]{1,0:T(8,128)}, f32[256,512]{1,0:T(8,128)S(1)}, u32[]{:S(2)}, u32[]{:S(2)}) collective-permute-start(f32[256,512]{1,0:T(8,128)} %get-tuple-element.81), channel_id=1, source_target_pairs={{0,0},{1,4},{2,1},{3,5},{4,2},{5,6},{6,3},{7,7},{8,11},{9,15},{10,... | collective-permute-start | bytes 1572872 | tf_op jit(solution)/shard_map/ppermute | solution.py:153
  47.2 32.2 %collective-permute-start.13 = (f32[256,512]{1,0:T(8,128)S(1)}, f32[256,512]{1,0:T(8,128)S(1)}, u32[]{:S(2)}, u32[]{:S(2)}) collective-permute-start(f32[256,512]{1,0:T(8,128)S(1)} %get-tuple-element.45.refs_0_.outer), channel_id=1, source_target_pairs={{4,1},{5,2},{6,3},{7,11},{15,10},{14,9},{13,8},{12,16},{20,17},{21... | collective-permute-start | bytes 1572872 | tf_op jit(solution)/shard_map/ppermute | solution.py:153
  47.9 31.5 %collective-permute-start.14 = (f32[256,512]{1,0:T(8,128)S(1)}, f32[256,512]{1,0:T(8,128)S(1)}, u32[]{:S(2)}, u32[]{:S(2)}) collective-permute-start(f32[256,512]{1,0:T(8,128)S(1)} %get-tuple-element.46.refs_1_.inner), channel_id=1, source_target_pairs={{0,4},{4,0},{1,5},{5,1},{2,6},{6,2},{3,7},{7,3},{11,15},{15,11},{1... | collective-permute-start | bytes 1572872 | tf_op jit(solution)/shard_map/ppermute | solution.py:153
  75.8 13.0 %collective-permute-start = (f32[256,512]{1,0:T(8,128)S(1)}, f32[256,512]{1,0:T(8,128)S(1)}, u32[]{:S(2)}, u32[]{:S(2)}) collective-permute-start(f32[256,512]{1,0:T(8,128)S(1)} %get-tuple-element.42), channel_id=1, source_target_pairs={{0,4},{1,5},{2,6},{3,7},{4,0},{5,1},{6,2},{7,3},{8,12},{9,13},{10,... | collective-permute-start | bytes 1572872 | tf_op jit(solution)/shard_map/ppermute | solution.py:153
  78.8 25.3 %collective-permute-start.12 = (f32[256,512]{1,0:T(8,128)S(1)}, f32[256,512]{1,0:T(8,128)S(1)}, u32[]{:S(2)}, u32[]{:S(2)}) collective-permute-start(f32[256,512]{1,0:T(8,128)S(1)} %get-tuple-element.48), channel_id=1, source_target_pairs={{0,4},{1,5},{2,6},{3,7},{4,0},{5,1},{6,2},{7,3},{8,12},{9,13},{10,... | collective-permute-start | bytes 1572872 | tf_op jit(solution)/shard_map/ppermute | solution.py:153
  81.4 14.0 %collective-permute-start.22 = (f32[256,512]{1,0:T(8,128)S(1)}, f32[256,512]{1,0:T(8,128)S(1)}, u32[]{:S(2)}, u32[]{:S(2)}) collective-permute-start(f32[256,512]{1,0:T(8,128)S(1)} %get-tuple-element.49.refs_0_.outer), channel_id=1, source_target_pairs={{4,1},{5,2},{6,3},{7,11},{15,10},{14,9},{13,8},{12,16},{20,17},{21... | collective-permute-start | bytes 1572872 | tf_op jit(solution)/shard_map/ppermute | solution.py:153
  82.1 17.7 %collective-permute-start.23 = (f32[256,512]{1,0:T(8,128)S(1)}, f32[256,512]{1,0:T(8,128)S(1)}, u32[]{:S(2)}, u32[]{:S(2)}) collective-permute-start(f32[256,512]{1,0:T(8,128)S(1)} %get-tuple-element.50.refs_1_.inner), channel_id=1, source_target_pairs={{0,4},{4,0},{1,5},{5,1},{2,6},{6,2},{3,7},{7,3},{11,15},{15,11},{1... | collective-permute-start | bytes 1572872 | tf_op jit(solution)/shard_map/ppermute | solution.py:153
  89.9 15.2 %collective-permute-start.15 = (f32[256,512]{1,0:T(8,128)S(1)}, f32[256,512]{1,0:T(8,128)S(1)}, u32[]{:S(2)}, u32[]{:S(2)}) collective-permute-start(f32[256,512]{1,0:T(8,128)S(1)} %get-tuple-element.52), channel_id=1, source_target_pairs={{0,4},{1,5},{2,6},{3,7},{4,0},{5,1},{6,2},{7,3},{8,12},{9,13},{10,... | collective-permute-start | bytes 1572872 | tf_op jit(solution)/shard_map/ppermute | solution.py:153
  90.0 19.9 %collective-permute-start.3 = (f32[1,64,512]{2,1,0:T(8,128)S(1)}, f32[1,64,512]{2,1,0:T(8,128)S(1)}, u32[]{:S(2)}, u32[]{:S(2)}) collective-permute-start(f32[1,64,512]{2,1,0:T(8,128)S(1)} %get-tuple-element.90), channel_id=1, source_target_pairs={{0,24},{1,25},{2,26},{3,27},{4,28},{5,29},{6,30},{7,31},{8,0},{9,1... | collective-permute-start | bytes 393224 | tf_op jit(solution)/shard_map/ppermute | solution.py:153
  95.4 14.5 %collective-permute-start.2 = (f32[1,64,512]{2,1,0:T(8,128)S(1)}, f32[1,64,512]{2,1,0:T(8,128)S(1)}, u32[]{:S(2)}, u32[]{:S(2)}) collective-permute-start(f32[1,64,512]{2,1,0:T(8,128)S(1)} %get-tuple-element.91), channel_id=1, source_target_pairs={{0,16},{1,17},{2,18},{3,19},{4,20},{5,21},{6,22},{7,23},{8,24},{9,... | collective-permute-start | bytes 393224 | tf_op jit(solution)/shard_map/ppermute | solution.py:153
  99.8 11.3 %collective-permute-start.1 = (f32[1,64,512]{2,1,0:T(8,128)S(1)}, f32[1,64,512]{2,1,0:T(8,128)S(1)}, u32[]{:S(2)}, u32[]{:S(2)}) collective-permute-start(f32[1,64,512]{2,1,0:T(8,128)S(1)} %get-tuple-element.89), channel_id=1, source_target_pairs={{0,8},{1,9},{2,10},{3,11},{4,12},{5,13},{6,14},{7,15},{8,16},{9,17... | collective-permute-start | bytes 393224 | tf_op jit(solution)/shard_map/ppermute | solution.py:153
  104.1 8.4 %collective-permute-start.25 = (f32[256,512]{1,0:T(8,128)S(1)}, f32[256,512]{1,0:T(8,128)S(1)}, u32[]{:S(2)}, u32[]{:S(2)}) collective-permute-start(f32[256,512]{1,0:T(8,128)S(1)} %get-tuple-element.53.refs_0_.outer), channel_id=1, source_target_pairs={{4,1},{5,2},{6,3},{7,11},{15,10},{14,9},{13,8},{12,16},{20,17},{21... | collective-permute-start | bytes 1572872 | tf_op jit(solution)/shard_map/ppermute | solution.py:153
  105.1 10.5 %collective-permute-start.26 = (f32[256,512]{1,0:T(8,128)S(1)}, f32[256,512]{1,0:T(8,128)S(1)}, u32[]{:S(2)}, u32[]{:S(2)}) collective-permute-start(f32[256,512]{1,0:T(8,128)S(1)} %get-tuple-element.54.refs_1_.inner), channel_id=1, source_target_pairs={{0,4},{4,0},{1,5},{5,1},{2,6},{6,2},{3,7},{7,3},{11,15},{15,11},{1... | collective-permute-start | bytes 1572872 | tf_op jit(solution)/shard_map/ppermute | solution.py:153
  109.9 9.2 %collective-permute-start.18 = (f32[2,64,512]{2,1,0:T(8,128)S(1)}, f32[2,64,512]{2,1,0:T(8,128)S(1)}, u32[]{:S(2)}, u32[]{:S(2)}) collective-permute-start(f32[2,64,512]{2,1,0:T(8,128)S(1)} %get-tuple-element.77), channel_id=1, source_target_pairs={{0,24},{1,25},{2,26},{3,27},{4,28},{5,29},{6,30},{7,31},{8,0},{9,1... | collective-permute-start | bytes 786440 | tf_op jit(solution)/shard_map/ppermute | solution.py:153
  110.0 13.9 %collective-permute-start.17 = (f32[2,64,512]{2,1,0:T(8,128)S(1)}, f32[2,64,512]{2,1,0:T(8,128)S(1)}, u32[]{:S(2)}, u32[]{:S(2)}) collective-permute-start(f32[2,64,512]{2,1,0:T(8,128)S(1)} %get-tuple-element.78), channel_id=1, source_target_pairs={{0,16},{1,17},{2,18},{3,19},{4,20},{5,21},{6,22},{7,23},{8,24},{9,... | collective-permute-start | bytes 786440 | tf_op jit(solution)/shard_map/ppermute | solution.py:153
  111.2 12.8 %collective-permute-start.16 = (f32[2,64,512]{2,1,0:T(8,128)S(1)}, f32[2,64,512]{2,1,0:T(8,128)S(1)}, u32[]{:S(2)}, u32[]{:S(2)}) collective-permute-start(f32[2,64,512]{2,1,0:T(8,128)S(1)} %get-tuple-element.76), channel_id=1, source_target_pairs={{0,8},{1,9},{2,10},{3,11},{4,12},{5,13},{6,14},{7,15},{8,16},{9,17... | collective-permute-start | bytes 786440 | tf_op jit(solution)/shard_map/ppermute | solution.py:153
  112.5 16.6 %collective-permute-start.24 = (f32[256,512]{1,0:T(8,128)S(1)}, f32[256,512]{1,0:T(8,128)S(1)}, u32[]{:S(2)}, u32[]{:S(2)}) collective-permute-start(f32[256,512]{1,0:T(8,128)S(1)} %get-tuple-element.56), channel_id=1, source_target_pairs={{0,4},{1,5},{2,6},{3,7},{4,0},{5,1},{6,2},{7,3},{8,12},{9,13},{10,... | collective-permute-start | bytes 1572872 | tf_op jit(solution)/shard_map/ppermute | solution.py:153
  118.7 10.6 %collective-permute-start.27 = (f32[256,512]{1,0:T(8,128)S(1)}, f32[256,512]{1,0:T(8,128)S(1)}, u32[]{:S(2)}, u32[]{:S(2)}) collective-permute-start(f32[256,512]{1,0:T(8,128)S(1)} %get-tuple-element.60), channel_id=1, source_target_pairs={{0,4},{1,5},{2,6},{3,7},{4,0},{5,1},{6,2},{7,3},{8,12},{9,13},{10,... | collective-permute-start | bytes 1572872 | tf_op jit(solution)/shard_map/ppermute | solution.py:153
  124.0 22.9 %collective-permute-start.19 = (f32[3,64,512]{2,1,0:T(8,128)S(1)}, f32[3,64,512]{2,1,0:T(8,128)S(1)}, u32[]{:S(2)}, u32[]{:S(2)}) collective-permute-start(f32[3,64,512]{2,1,0:T(8,128)S(1)} %pad_maximum_fusion), channel_id=1, source_target_pairs={{0,1},{4,5},{8,9},{12,13},{16,17},{20,21},{24,25},{28,29},{3,2},{7... | collective-permute-start | bytes 1179656 | tf_op jit(solution)/shard_map/ppermute | solution.py:153
  127.7 6.9 %collective-permute-start.34 = (f32[256,512]{1,0:T(8,128)S(1)}, f32[256,512]{1,0:T(8,128)S(1)}, u32[]{:S(2)}, u32[]{:S(2)}) collective-permute-start(f32[256,512]{1,0:T(8,128)S(1)} %get-tuple-element.57.refs_0_.outer), channel_id=1, source_target_pairs={{4,1},{5,2},{6,3},{7,11},{15,10},{14,9},{13,8},{12,16},{20,17},{21... | collective-permute-start | bytes 1572872 | tf_op jit(solution)/shard_map/ppermute | solution.py:153
  128.4 14.7 %collective-permute-start.35 = (f32[256,512]{1,0:T(8,128)S(1)}, f32[256,512]{1,0:T(8,128)S(1)}, u32[]{:S(2)}, u32[]{:S(2)}) collective-permute-start(f32[256,512]{1,0:T(8,128)S(1)} %get-tuple-element.58.refs_1_.inner), channel_id=1, source_target_pairs={{0,4},{4,0},{1,5},{5,1},{2,6},{6,2},{3,7},{7,3},{11,15},{15,11},{1... | collective-permute-start | bytes 1572872 | tf_op jit(solution)/shard_map/ppermute | solution.py:153
  129.4 19.7 %collective-permute-start.30 = (f32[2,64,512]{2,1,0:T(8,128)S(1)}, f32[2,64,512]{2,1,0:T(8,128)S(1)}, u32[]{:S(2)}, u32[]{:S(2)}) collective-permute-start(f32[2,64,512]{2,1,0:T(8,128)S(1)} %get-tuple-element.74), channel_id=1, source_target_pairs={{0,24},{1,25},{2,26},{3,27},{4,28},{5,29},{6,30},{7,31},{8,0},{9,1... | collective-permute-start | bytes 786440 | tf_op jit(solution)/shard_map/ppermute | solution.py:153
  131.3 17.9 %collective-permute-start.29 = (f32[2,64,512]{2,1,0:T(8,128)S(1)}, f32[2,64,512]{2,1,0:T(8,128)S(1)}, u32[]{:S(2)}, u32[]{:S(2)}) collective-permute-start(f32[2,64,512]{2,1,0:T(8,128)S(1)} %get-tuple-element.75), channel_id=1, source_target_pairs={{0,16},{1,17},{2,18},{3,19},{4,20},{5,21},{6,22},{7,23},{8,24},{9,... | collective-permute-start | bytes 786440 | tf_op jit(solution)/shard_map/ppermute | solution.py:153
  134.5 15.3 %collective-permute-start.28 = (f32[2,64,512]{2,1,0:T(8,128)S(1)}, f32[2,64,512]{2,1,0:T(8,128)S(1)}, u32[]{:S(2)}, u32[]{:S(2)}) collective-permute-start(f32[2,64,512]{2,1,0:T(8,128)S(1)} %get-tuple-element.73), channel_id=1, source_target_pairs={{0,8},{1,9},{2,10},{3,11},{4,12},{5,13},{6,14},{7,15},{8,16},{9,17... | collective-permute-start | bytes 786440 | tf_op jit(solution)/shard_map/ppermute | solution.py:153
  146.9 18.5 %collective-permute-start.36 = (f32[256,512]{1,0:T(8,128)}, f32[256,512]{1,0:T(8,128)}, u32[]{:S(2)}, u32[]{:S(2)}) collective-permute-start(f32[256,512]{1,0:T(8,128)} %get-tuple-element.64), channel_id=1, source_target_pairs={{0,4},{1,5},{2,6},{3,7},{4,0},{5,1},{6,2},{7,3},{8,12},{9,13},{10,... | collective-permute-start | bytes 1572872 | tf_op jit(solution)/shard_map/ppermute | solution.py:153
  147.7 11.5 %collective-permute-start.20 = (f32[3,64,512]{2,1,0:T(8,128)}, f32[3,64,512]{2,1,0:T(8,128)}, u32[]{:S(2)}, u32[]{:S(2)}) collective-permute-start(f32[3,64,512]{2,1,0:T(8,128)} %fusion.18), channel_id=1, source_target_pairs={{1,2},{5,6},{9,10},{13,14},{17,18},{21,22},{25,26},{29,30},{2,1},{... | collective-permute-start | bytes 1179656 | tf_op jit(solution)/shard_map/ppermute | solution.py:153
  150.6 13.0 %collective-permute-start.31 = (f32[2,64,512]{2,1,0:T(8,128)}, f32[2,64,512]{2,1,0:T(8,128)}, u32[]{:S(2)}, u32[]{:S(2)}) collective-permute-start(f32[2,64,512]{2,1,0:T(8,128)} %fusion.4), channel_id=1, source_target_pairs={{0,1},{4,5},{8,9},{12,13},{16,17},{20,21},{24,25},{28,29},{3,2},{7... | collective-permute-start | bytes 786440 | tf_op jit(solution)/shard_map/ppermute | solution.py:153
  157.3 9.3 %collective-permute-start.43 = (f32[256,512]{1,0:T(8,128)S(1)}, f32[256,512]{1,0:T(8,128)S(1)}, u32[]{:S(2)}, u32[]{:S(2)}) collective-permute-start(f32[256,512]{1,0:T(8,128)S(1)} %get-tuple-element.61.refs_0_.outer), channel_id=1, source_target_pairs={{4,1},{5,2},{6,3},{7,11},{15,10},{14,9},{13,8},{12,16},{20,17},{21... | collective-permute-start | bytes 1572872 | tf_op jit(solution)/shard_map/ppermute | solution.py:153
  158.0 11.2 %collective-permute-start.44 = (f32[256,512]{1,0:T(8,128)S(1)}, f32[256,512]{1,0:T(8,128)S(1)}, u32[]{:S(2)}, u32[]{:S(2)}) collective-permute-start(f32[256,512]{1,0:T(8,128)S(1)} %get-tuple-element.62.refs_1_.inner), channel_id=1, source_target_pairs={{0,4},{4,0},{1,5},{5,1},{2,6},{6,2},{3,7},{7,3},{11,15},{15,11},{1... | collective-permute-start | bytes 1572872 | tf_op jit(solution)/shard_map/ppermute | solution.py:153
  160.4 21.7 %collective-permute-start.21 = (f32[3,64,512]{2,1,0:T(8,128)S(1)}, f32[3,64,512]{2,1,0:T(8,128)S(1)}, u32[]{:S(2)}, u32[]{:S(2)}) collective-permute-start(f32[3,64,512]{2,1,0:T(8,128)S(1)} %add.128), channel_id=1, source_target_pairs={{1,0},{5,4},{9,8},{13,12},{17,16},{21,20},{25,24},{29,28}} | collective-permute-start | bytes 1179656 | tf_op jit(solution)/shard_map/ppermute | solution.py:153
  164.7 20.6 %collective-permute-start.32 = (f32[2,64,512]{2,1,0:T(8,128)S(1)}, f32[2,64,512]{2,1,0:T(8,128)S(1)}, u32[]{:S(2)}, u32[]{:S(2)}) collective-permute-start(f32[2,64,512]{2,1,0:T(8,128)S(1)} %add.134), channel_id=1, source_target_pairs={{1,2},{5,6},{9,10},{13,14},{17,18},{21,22},{25,26},{29,30},{2,1},{... | collective-permute-start | bytes 786440 | tf_op jit(solution)/shard_map/ppermute | solution.py:153
  166.6 9.4 %collective-permute-start.38 = (f32[1,64,512]{2,1,0:T(8,128)S(1)}, f32[1,64,512]{2,1,0:T(8,128)S(1)}, u32[]{:S(2)}, u32[]{:S(2)}) collective-permute-start(f32[1,64,512]{2,1,0:T(8,128)S(1)} %get-tuple-element.88), channel_id=1, source_target_pairs={{0,16},{1,17},{2,18},{3,19},{4,20},{5,21},{6,22},{7,23},{8,24},{9,... | collective-permute-start | bytes 393224 | tf_op jit(solution)/shard_map/ppermute | solution.py:153
  169.2 6.8 %collective-permute-start.37 = (f32[1,64,512]{2,1,0:T(8,128)S(1)}, f32[1,64,512]{2,1,0:T(8,128)S(1)}, u32[]{:S(2)}, u32[]{:S(2)}) collective-permute-start(f32[1,64,512]{2,1,0:T(8,128)S(1)} %get-tuple-element.86), channel_id=1, source_target_pairs={{0,8},{1,9},{2,10},{3,11},{4,12},{5,13},{6,14},{7,15},{8,16},{9,17... | collective-permute-start | bytes 393224 | tf_op jit(solution)/shard_map/ppermute | solution.py:153
  172.3 15.1 %collective-permute-start.45 = (f32[256,512]{1,0:T(8,128)S(1)}, f32[256,512]{1,0:T(8,128)S(1)}, u32[]{:S(2)}, u32[]{:S(2)}) collective-permute-start(f32[256,512]{1,0:T(8,128)S(1)} %get-tuple-element.68), channel_id=1, source_target_pairs={{0,4},{1,5},{2,6},{3,7},{4,0},{5,1},{6,2},{7,3},{8,12},{9,13},{10,... | collective-permute-start | bytes 1572872 | tf_op jit(solution)/shard_map/ppermute | solution.py:153
  176.0 8.6 %collective-permute-start.40 = (f32[1,64,512]{2,1,0:T(8,128)S(1)}, f32[1,64,512]{2,1,0:T(8,128)S(1)}, u32[]{:S(2)}, u32[]{:S(2)}) collective-permute-start(f32[1,64,512]{2,1,0:T(8,128)S(1)} %fusion.15), channel_id=1, source_target_pairs={{0,1},{4,5},{8,9},{12,13},{16,17},{20,21},{24,25},{28,29},{3,2},{7... | collective-permute-start | bytes 393224 | tf_op jit(solution)/shard_map/ppermute | solution.py:153
  185.4 11.0 %collective-permute-start.33 = (f32[2,64,512]{2,1,0:T(8,128)S(1)}, f32[2,64,512]{2,1,0:T(8,128)S(1)}, u32[]{:S(2)}, u32[]{:S(2)}) collective-permute-start(f32[2,64,512]{2,1,0:T(8,128)S(1)} %add.135), channel_id=1, source_target_pairs={{1,0},{5,4},{9,8},{13,12},{17,16},{21,20},{25,24},{29,28},{2,3},{6... | collective-permute-start | bytes 786440 | tf_op jit(solution)/shard_map/ppermute | solution.py:153
  186.7 16.9 %collective-permute-start.42 = (f32[1,64,512]{2,1,0:T(8,128)S(1)}, f32[1,64,512]{2,1,0:T(8,128)S(1)}, u32[]{:S(2)}, u32[]{:S(2)}) collective-permute-start(f32[1,64,512]{2,1,0:T(8,128)S(1)} %add.141), channel_id=1, source_target_pairs={{2,3},{6,7},{10,11},{14,15},{18,19},{22,23},{26,27},{30,31}} | collective-permute-start | bytes 393224 | tf_op jit(solution)/shard_map/ppermute | solution.py:153
  187.5 8.9 %collective-permute-start.48 = (f32[1,64,512]{2,1,0:T(8,128)S(1)}, f32[1,64,512]{2,1,0:T(8,128)S(1)}, u32[]{:S(2)}, u32[]{:S(2)}) collective-permute-start(f32[1,64,512]{2,1,0:T(8,128)S(1)} %get-tuple-element.84), channel_id=1, source_target_pairs={{0,24},{1,25},{2,26},{3,27},{4,28},{5,29},{6,30},{7,31},{8,0},{9,1... | collective-permute-start | bytes 393224 | tf_op jit(solution)/shard_map/ppermute | solution.py:153
  188.4 8.1 %collective-permute-start.47 = (f32[1,64,512]{2,1,0:T(8,128)S(1)}, f32[1,64,512]{2,1,0:T(8,128)S(1)}, u32[]{:S(2)}, u32[]{:S(2)}) collective-permute-start(f32[1,64,512]{2,1,0:T(8,128)S(1)} %get-tuple-element.85), channel_id=1, source_target_pairs={{0,16},{1,17},{2,18},{3,19},{4,20},{5,21},{6,22},{7,23},{8,24},{9,... | collective-permute-start | bytes 393224 | tf_op jit(solution)/shard_map/ppermute | solution.py:153
  189.7 6.8 %collective-permute-start.46 = (f32[1,64,512]{2,1,0:T(8,128)S(1)}, f32[1,64,512]{2,1,0:T(8,128)S(1)}, u32[]{:S(2)}, u32[]{:S(2)}) collective-permute-start(f32[1,64,512]{2,1,0:T(8,128)S(1)} %get-tuple-element.83), channel_id=1, source_target_pairs={{0,8},{1,9},{2,10},{3,11},{4,12},{5,13},{6,14},{7,15},{8,16},{9,17... | collective-permute-start | bytes 393224 | tf_op jit(solution)/shard_map/ppermute | solution.py:153
  196.6 7.1 %collective-permute-start.51 = (f32[1,64,512]{2,1,0:T(8,128)S(1)}, f32[1,64,512]{2,1,0:T(8,128)S(1)}, u32[]{:S(2)}, u32[]{:S(2)}) collective-permute-start(f32[1,64,512]{2,1,0:T(8,128)S(1)} %fusion.13), channel_id=1, source_target_pairs={{2,3},{6,7},{10,11},{14,15},{18,19},{22,23},{26,27},{30,31}} | collective-permute-start | bytes 393224 | tf_op jit(solution)/shard_map/ppermute | solution.py:153
  197.2 6.5 %collective-permute-start.50 = (f32[1,64,512]{2,1,0:T(8,128)S(1)}, f32[1,64,512]{2,1,0:T(8,128)S(1)}, u32[]{:S(2)}, u32[]{:S(2)}) collective-permute-start(f32[1,64,512]{2,1,0:T(8,128)S(1)} %fusion.13), channel_id=1, source_target_pairs={{1,3},{5,7},{9,11},{13,15},{17,19},{21,23},{25,27},{29,31}} | collective-permute-start | bytes 393224 | tf_op jit(solution)/shard_map/ppermute | solution.py:153
  197.9 8.2 %collective-permute-start.49 = (f32[1,64,512]{2,1,0:T(8,128)S(1)}, f32[1,64,512]{2,1,0:T(8,128)S(1)}, u32[]{:S(2)}, u32[]{:S(2)}) collective-permute-start(f32[1,64,512]{2,1,0:T(8,128)S(1)} %fusion.13), channel_id=1, source_target_pairs={{0,3},{4,7},{8,11},{12,15},{16,19},{20,23},{24,27},{28,31}} | collective-permute-start | bytes 393224 | tf_op jit(solution)/shard_map/ppermute | solution.py:153
  207.6 6.4 %collective-permute-start.53 = (f32[64,512]{1,0:T(8,128)S(1)}, f32[64,512]{1,0:T(8,128)S(1)}, u32[]{:S(2)}, u32[]{:S(2)}) collective-permute-start(f32[64,512]{1,0:T(8,128)S(1)} %get-tuple-element.71), channel_id=1, source_target_pairs={{0,16},{1,17},{2,18},{3,19},{4,20},{5,21},{6,22},{7,23},{8,24},{9,... | collective-permute-start | bytes 393224 | tf_op jit(solution)/shard_map/ppermute | solution.py:153
  (14 other events, 271.6 us)
where the time goes:
time: 219 us; the launch traced here: 216 us
  starting transfers between devices  155 us (71%)
  Pallas kernels  26.6 us (12%)
  waiting for transfers between devices  25 us (11%)
  other arithmetic  6.05 us (3%)
  local copies, waits for them, and re-layouts  2.64 us (1%)
    ppermute x55, starting transfers between devices, permute(): return lax.ppermute(x, AXES, pairs)  155 us
    pallas_call x17, Pallas kernels, call(): pl.pallas_call(kernel, out_shape=outs, in_specs=specs, out_specs=jax.tree...  26.6 us
    ppermute x55, waiting for transfers between devices, permute(): return lax.ppermute(x, AXES, pairs)  25 us
  transfers between devices with their start and end apart: 55, of which 11 were waited for; matrix products, arithmetic and copies ran while one was open for 3% of the time, Pallas kernels for 11%

commit v1 on v0

--- a/solution.py
+++ b/solution.py
@@ -170,20 +170,19 @@
     width = ctrl.shape[1]
     quarter = width // (parts * ORDERS)
 
-    def halves(x):
-        first = (c % 2) * margin
+    def halves(x, odd):
+        first = odd * margin
         return (
             lax.dynamic_slice_in_dim(x, first, margin, 0),
             lax.dynamic_slice_in_dim(x, margin - first, margin, 0),
         )
 
-    first, second = halves(ctrl)
-    far_first, far_second = halves(obsv)
+    moved_ctrl = permute(ctrl, relay)
     moved_offs = permute(offs, relay)
-    outer = permute(first, relay)
-    inner = permute(second, relay)
     moved_tiles = permute(tiles, relay)
-    far = (permute(far_first, relay), permute(far_second, relay))
+    far_halves = halves(obsv, c % 2)
+    far = tuple(permute(x, relay) for x in far_halves)
+    outer, inner = halves(moved_ctrl, r % 2)
     near_turned = turn(parts, pos, (obsv,))
     far_turned = turn(parts, pos, far)
 

time: 219 us -> 222 us (1.014)
  waiting for transfers between devices: 25 us -> 39.9 us
  starting transfers between devices: 155 us -> 143 us
    ppermute x55 -> x54, waiting for transfers between devices: 25 us -> 39.9 us  [permute(): return lax.ppermute(x, AXES, pairs)]
    ppermute x55 -> x54, starting transfers between devices: 155 us -> 143 us  [permute(): return lax.ppermute(x, AXES, pairs)]
  transfers between devices with their start and end apart: 55 -> 54, of which waited for: 11 -> 10; matrix products, arithmetic and copies ran while one was open for 3% -> 4% of each run, Pallas kernels for 11% -> 11%
where the time goes in v1:
time: 222 us; the launch traced here: 219 us
  starting transfers between devices  143 us (64%)
  waiting for transfers between devices  39.9 us (18%)
  Pallas kernels  26.3 us (12%)
  other arithmetic  6.29 us (3%)
  local copies, waits for them, and re-layouts  2.75 us (1%)
    ppermute x54, starting transfers between devices, permute(): return lax.ppermute(x, AXES, pairs)  143 us
    ppermute x54, waiting for transfers between devices, permute(): return lax.ppermute(x, AXES, pairs)  39.9 us
    pallas_call x17, Pallas kernels, call(): pl.pallas_call(kernel, out_shape=outs, in_specs=specs, out_specs=jax.tree...  26.3 us
  transfers between devices with their start and end apart: 54, of which 10 were waited for; matrix products, arithmetic and copies ran while one was open for 4% of the time, Pallas kernels for 11%

profile of v1, /device:TPU:0, one launch (start us, length us, event | category | flops | bytes accessed | tf_op | source)
XLA Modules:
  0.0 218.6 jit_solution(16711431145377910105)
XLA Ops:
  0.0 9.4 %collective-permute-start.7 = (f32[512,512]{1,0:T(8,128)}, f32[512,512]{1,0:T(8,128)}, u32[]{:S(2)}, u32[]{:S(2)}) collective-permute-start(f32[512,512]{1,0:T(8,128)} %refs_0_.3), channel_id=1, source_target_pairs={{0,0},{1,4},{2,1},{3,5},{4,2},{5,6},{6,3},{7,7},{8,11},{9,15},{10,... | collective-permute-start | bytes 3145736 | tf_op jit(solution)/shard_map/ppermute | solution.py:153
  9.4 1.8 collective-permute-start.10
  11.2 1.4 constant_dynamic-slice_fusion
  12.6 1.5 collective-permute-start.8
  14.1 29.0 %collective-permute-start.9 = (f32[256,512]{1,0:T(8,128)S(1)}, f32[256,512]{1,0:T(8,128)}, u32[]{:S(2)}, u32[]{:S(2)}) collective-permute-start(f32[256,512]{1,0:T(8,128)S(1)} %get-tuple-element.79.inner), channel_id=1, source_target_pairs={{0,4},{4,0},{1,5},{5,1},{2,6},{6,2},{3,7},{7,3},{11,15},{15,11},{1... | collective-permute-start | bytes 1572872 | tf_op jit(solution)/shard_map/ppermute | solution.py:153
  44.1 1.7 collective-permute-start.4
  46.5 5.4 %collective-permute-start.5 = (f32[256,512]{1,0:T(8,128)}, f32[256,512]{1,0:T(8,128)}, u32[]{:S(2)}, u32[]{:S(2)}) collective-permute-start(f32[256,512]{1,0:T(8,128)} %get-tuple-element.81), channel_id=1, source_target_pairs={{0,0},{1,4},{2,1},{3,5},{4,2},{5,6},{6,3},{7,7},{8,11},{9,15},{10,... | collective-permute-start | bytes 1572872 | tf_op jit(solution)/shard_map/ppermute | solution.py:153
  51.9 2.7 %shard_map.49 = (f32[256,512]{1,0:T(8,128)S(1)}, f32[256,512]{1,0:T(8,128)S(1)}) custom-call(s32[4,3]{1,0:T(4,128)S(1)} %collective-permute-done.6.offs, s32[5]{0:T(128)S(1)} %stack.44.pos, f32[256,512]{1,0:T(8,128)S(1)} %get-tuple-element.80.outer, f32[256,512]{1,0:T(8,128)S(1)} %get-tuple-element.79.inner, f32[256,512]{1,0:T(8,128)} %collective-permute-done.8.from_outer, ...), custom_call_target="tpu_custom_call" | custom-call | flops 603979776 | bytes 4194304 | tf_op jit(solution)/shard_map/pallas_call | solution.py:25
  55.5 16.4 %collective-permute-start.13 = (f32[256,512]{1,0:T(8,128)S(1)}, f32[256,512]{1,0:T(8,128)S(1)}, u32[]{:S(2)}, u32[]{:S(2)}) collective-permute-start(f32[256,512]{1,0:T(8,128)S(1)} %get-tuple-element.46.refs_1_.inner), channel_id=1, source_target_pairs={{0,4},{4,0},{1,5},{5,1},{2,6},{6,2},{3,7},{7,3},{11,15},{15,11},{1... | collective-permute-start | bytes 1572872 | tf_op jit(solution)/shard_map/ppermute | solution.py:153
  71.9 1.9 shard_map.46
  74.9 2.4 %shard_map.48 = (bf16[512,512]{1,0:T(8,128)(2,1)S(1)}, bf16[512,512]{1,0:T(8,128)(2,1)S(1)}) custom-call(s32[5]{0:T(128)S(1)} %stack.44.pos, f32[256,512]{1,0:T(8,128)S(1)} %collective-permute-done.4.refs_0_, f32[256,512]{1,0:T(8,128)} %collective-permute-done.5.refs_1_), custom_call_target="tpu_custom_call" | custom-call | flops 262144 | bytes 2097152 | tf_op jit(solution)/shard_map/pallas_call | solution.py:25
  78.9 2.0 shard_map.51
  83.6 7.7 %collective-permute-start.22 = (f32[256,512]{1,0:T(8,128)S(1)}, f32[256,512]{1,0:T(8,128)S(1)}, u32[]{:S(2)}, u32[]{:S(2)}) collective-permute-start(f32[256,512]{1,0:T(8,128)S(1)} %get-tuple-element.50.refs_1_.inner), channel_id=1, source_target_pairs={{0,4},{4,0},{1,5},{5,1},{2,6},{6,2},{3,7},{7,3},{11,15},{15,11},{1... | collective-permute-start | bytes 1572872 | tf_op jit(solution)/shard_map/ppermute | solution.py:153
  91.5 4.0 %collective-permute-start.17 = (f32[2,64,512]{2,1,0:T(8,128)S(1)}, f32[2,64,512]{2,1,0:T(8,128)S(1)}, u32[]{:S(2)}, u32[]{:S(2)}) collective-permute-start(f32[2,64,512]{2,1,0:T(8,128)S(1)} %get-tuple-element.77), channel_id=1, source_target_pairs={{0,24},{1,25},{2,26},{3,27},{4,28},{5,29},{6,30},{7,31},{8,0},{9,1... | collective-permute-start | bytes 786440 | tf_op jit(solution)/shard_map/ppermute | solution.py:153
  96.2 4.8 %collective-permute-start.1 = (f32[1,64,512]{2,1,0:T(8,128)S(1)}, f32[1,64,512]{2,1,0:T(8,128)S(1)}, u32[]{:S(2)}, u32[]{:S(2)}) collective-permute-start(f32[1,64,512]{2,1,0:T(8,128)S(1)} %get-tuple-element.89), channel_id=1, source_target_pairs={{0,8},{1,9},{2,10},{3,11},{4,12},{5,13},{6,14},{7,15},{8,16},{9,17... | collective-permute-start | bytes 393224 | tf_op jit(solution)/shard_map/ppermute | solution.py:153
  101.0 1.9 collective-permute-start.16
  102.9 2.1 shard_map.53
  105.0 7.4 %collective-permute-start.15 = (f32[2,64,512]{2,1,0:T(8,128)S(1)}, f32[2,64,512]{2,1,0:T(8,128)S(1)}, u32[]{:S(2)}, u32[]{:S(2)}) collective-permute-start(f32[2,64,512]{2,1,0:T(8,128)S(1)} %get-tuple-element.76), channel_id=1, source_target_pairs={{0,8},{1,9},{2,10},{3,11},{4,12},{5,13},{6,14},{7,15},{8,16},{9,17... | collective-permute-start | bytes 786440 | tf_op jit(solution)/shard_map/ppermute | solution.py:153
  114.8 8.0 %collective-permute-done.16 = f32[2,64,512]{2,1,0:T(8,128)S(1)} collective-permute-done((f32[2,64,512]{2,1,0:T(8,128)S(1)}, f32[2,64,512]{2,1,0:T(8,128)S(1)}, u32[]{:S(2)}, u32[]{:S(2)}) %collective-permute-start.16) | collective-permute-done | bytes 262176 | tf_op jit(solution)/shard_map/ppermute | solution.py:153
  122.9 1.3 collective-permute-start.18
  124.3 2.1 shard_map.55
  127.1 2.2 %collective-permute-start.34 = (f32[256,512]{1,0:T(8,128)S(1)}, f32[256,512]{1,0:T(8,128)S(1)}, u32[]{:S(2)}, u32[]{:S(2)}) collective-permute-start(f32[256,512]{1,0:T(8,128)S(1)} %get-tuple-element.58.refs_1_.inner), channel_id=1, source_target_pairs={{0,4},{4,0},{1,5},{5,1},{2,6},{6,2},{3,7},{7,3},{11,15},{15,11},{1... | collective-permute-start | bytes 1572872 | tf_op jit(solution)/shard_map/ppermute | solution.py:153
  130.5 3.0 %collective-permute-done.18 = f32[3,64,512]{2,1,0:T(8,128)S(1)} collective-permute-done((f32[3,64,512]{2,1,0:T(8,128)S(1)}, f32[3,64,512]{2,1,0:T(8,128)S(1)}, u32[]{:S(2)}, u32[]{:S(2)}) %collective-permute-start.18) | collective-permute-done | bytes 393248 | tf_op jit(solution)/shard_map/ppermute | solution.py:153
  134.3 1.4 collective-permute-start.19
  135.7 2.0 shard_map.57
  138.7 3.9 %collective-permute-start.35 = (f32[256,512]{1,0:T(8,128)S(1)}, f32[256,512]{1,0:T(8,128)}, u32[]{:S(2)}, u32[]{:S(2)}) collective-permute-start(f32[256,512]{1,0:T(8,128)S(1)} %get-tuple-element.64), channel_id=1, source_target_pairs={{0,4},{1,5},{2,6},{3,7},{4,0},{5,1},{6,2},{7,3},{8,12},{9,13},{10,... | collective-permute-start | bytes 1572872 | tf_op jit(solution)/shard_map/ppermute | solution.py:153
  143.8 2.4 %collective-permute-start.28 = (f32[2,64,512]{2,1,0:T(8,128)}, f32[2,64,512]{2,1,0:T(8,128)}, u32[]{:S(2)}, u32[]{:S(2)}) collective-permute-start(f32[2,64,512]{2,1,0:T(8,128)} %get-tuple-element.75), channel_id=1, source_target_pairs={{0,16},{1,17},{2,18},{3,19},{4,20},{5,21},{6,22},{7,23},{8,24},{9,... | collective-permute-start | bytes 786440 | tf_op jit(solution)/shard_map/ppermute | solution.py:153
  146.2 2.0 collective-permute-start.27
  149.1 1.2 add.135
  150.3 3.0 %collective-permute-done.29 = f32[2,64,512]{2,1,0:T(8,128)} collective-permute-done((f32[2,64,512]{2,1,0:T(8,128)}, f32[2,64,512]{2,1,0:T(8,128)}, u32[]{:S(2)}, u32[]{:S(2)}) %collective-permute-start.29) | collective-permute-done | bytes 262176 | tf_op jit(solution)/shard_map/ppermute | solution.py:153
  154.1 9.5 %collective-permute-done.28 = f32[2,64,512]{2,1,0:T(8,128)} collective-permute-done((f32[2,64,512]{2,1,0:T(8,128)}, f32[2,64,512]{2,1,0:T(8,128)}, u32[]{:S(2)}, u32[]{:S(2)}) %collective-permute-start.28) | collective-permute-done | bytes 262176 | tf_op jit(solution)/shard_map/ppermute | solution.py:153
  163.6 1.3 collective-permute-start.20
  164.9 1.2 fusion.4
  166.1 4.6 %collective-permute-start.30 = (f32[2,64,512]{2,1,0:T(8,128)S(1)}, f32[2,64,512]{2,1,0:T(8,128)S(1)}, u32[]{:S(2)}, u32[]{:S(2)}) collective-permute-start(f32[2,64,512]{2,1,0:T(8,128)S(1)} %fusion.4), channel_id=1, source_target_pairs={{0,1},{4,5},{8,9},{12,13},{16,17},{20,21},{24,25},{28,29},{3,2},{7... | collective-permute-start | bytes 786440 | tf_op jit(solution)/shard_map/ppermute | solution.py:153
  170.7 1.1 add_bitcast_fusion.1
  171.9 2.5 %collective-permute-start.37 = (f32[1,64,512]{2,1,0:T(8,128)S(1)}, f32[1,64,512]{2,1,0:T(8,128)S(1)}, u32[]{:S(2)}, u32[]{:S(2)}) collective-permute-start(f32[1,64,512]{2,1,0:T(8,128)S(1)} %get-tuple-element.88), channel_id=1, source_target_pairs={{0,16},{1,17},{2,18},{3,19},{4,20},{5,21},{6,22},{7,23},{8,24},{9,... | collective-permute-start | bytes 393224 | tf_op jit(solution)/shard_map/ppermute | solution.py:153
  174.5 1.9 collective-permute-start.36
  176.4 2.0 shard_map.59
  180.4 2.5 %collective-permute-start.39 = (f32[1,64,512]{2,1,0:T(8,128)S(1)}, f32[1,64,512]{2,1,0:T(8,128)S(1)}, u32[]{:S(2)}, u32[]{:S(2)}) collective-permute-start(f32[1,64,512]{2,1,0:T(8,128)S(1)} %fusion.15), channel_id=1, source_target_pairs={{0,1},{4,5},{8,9},{12,13},{16,17},{20,21},{24,25},{28,29},{3,2},{7... | collective-permute-start | bytes 393224 | tf_op jit(solution)/shard_map/ppermute | solution.py:153
  183.0 3.3 %collective-permute-done.39 = f32[1,64,512]{2,1,0:T(8,128)S(1)} collective-permute-done((f32[1,64,512]{2,1,0:T(8,128)S(1)}, f32[1,64,512]{2,1,0:T(8,128)S(1)}, u32[]{:S(2)}, u32[]{:S(2)}) %collective-permute-start.39) | collective-permute-done | bytes 131104 | tf_op jit(solution)/shard_map/ppermute | solution.py:153
  187.1 1.3 collective-permute-start.32
  191.9 7.5 %collective-permute-done.32 = f32[2,64,512]{2,1,0:T(8,128)S(1)} collective-permute-done((f32[2,64,512]{2,1,0:T(8,128)S(1)}, f32[2,64,512]{2,1,0:T(8,128)S(1)}, u32[]{:S(2)}, u32[]{:S(2)}) %collective-permute-start.32) | collective-permute-done | bytes 262176 | tf_op jit(solution)/shard_map/ppermute | solution.py:153
  200.8 6.6 %collective-permute-start.48 = (f32[1,64,512]{2,1,0:T(8,128)S(1)}, f32[1,64,512]{2,1,0:T(8,128)S(1)}, u32[]{:S(2)}, u32[]{:S(2)}) collective-permute-start(f32[1,64,512]{2,1,0:T(8,128)S(1)} %fusion.13), channel_id=1, source_target_pairs={{0,3},{4,7},{8,11},{12,15},{16,19},{20,23},{24,27},{28,31}} | collective-permute-start | bytes 393224 | tf_op jit(solution)/shard_map/ppermute | solution.py:153
  207.5 2.5 %collective-permute-done.48 = f32[1,64,512]{2,1,0:T(8,128)S(1)} collective-permute-done((f32[1,64,512]{2,1,0:T(8,128)S(1)}, f32[1,64,512]{2,1,0:T(8,128)S(1)}, u32[]{:S(2)}, u32[]{:S(2)}) %collective-permute-start.48) | collective-permute-done | bytes 131104 | tf_op jit(solution)/shard_map/ppermute | solution.py:153
  210.8 1.5 collective-permute-start.52
  212.3 2.0 collective-permute-start.53
  214.2 2.5 %collective-permute-done.51.refs_1_ = f32[64,512]{1,0:T(8,128)S(1)} collective-permute-done((f32[64,512]{1,0:T(8,128)S(1)}, f32[64,512]{1,0:T(8,128)S(1)}, u32[]{:S(2)}, u32[]{:S(2)}) %collective-permute-start.51) | collective-permute-done | bytes 131104 | tf_op jit(solution)/shard_map/ppermute | solution.py:153
  217.2 1.4 shard_map.62
  (132 shorter events, 26.6 us)
Async XLA Ops:
  0.0 11.2 %collective-permute-start.7 = (f32[512,512]{1,0:T(8,128)}, f32[512,512]{1,0:T(8,128)}, u32[]{:S(2)}, u32[]{:S(2)}) collective-permute-start(f32[512,512]{1,0:T(8,128)} %refs_0_.3), channel_id=1, source_target_pairs={{0,0},{1,4},{2,1},{3,5},{4,2},{5,6},{6,3},{7,7},{8,11},{9,15},{10,... | collective-permute-start | bytes 3145736 | tf_op jit(solution)/shard_map/ppermute | solution.py:153
  9.4 42.5 %collective-permute-start.10 = (f32[512,384]{1,0:T(8,128)}, f32[512,384]{1,0:T(8,128)S(1)}, u32[]{:S(2)}, u32[]{:S(2)}) collective-permute-start(f32[512,384]{1,0:T(8,128)} %param.6), channel_id=1, source_target_pairs={{0,0},{1,4},{2,1},{3,5},{4,2},{5,6},{6,3},{7,7},{8,11},{9,15},{10,... | collective-permute-start | bytes 2359304 | tf_op jit(solution)/shard_map/ppermute | solution.py:153
  12.6 39.3 %collective-permute-start.8 = (f32[256,512]{1,0:T(8,128)S(1)}, f32[256,512]{1,0:T(8,128)}, u32[]{:S(2)}, u32[]{:S(2)}) collective-permute-start(f32[256,512]{1,0:T(8,128)S(1)} %get-tuple-element.80.outer), channel_id=1, source_target_pairs={{4,1},{5,2},{6,3},{7,11},{15,10},{14,9},{13,8},{12,16},{20,17},{21... | collective-permute-start | bytes 1572872 | tf_op jit(solution)/shard_map/ppermute | solution.py:153
  14.1 37.9 %collective-permute-start.9 = (f32[256,512]{1,0:T(8,128)S(1)}, f32[256,512]{1,0:T(8,128)}, u32[]{:S(2)}, u32[]{:S(2)}) collective-permute-start(f32[256,512]{1,0:T(8,128)S(1)} %get-tuple-element.79.inner), channel_id=1, source_target_pairs={{0,4},{4,0},{1,5},{5,1},{2,6},{6,2},{3,7},{7,3},{11,15},{15,11},{1... | collective-permute-start | bytes 1572872 | tf_op jit(solution)/shard_map/ppermute | solution.py:153
  44.1 30.8 %collective-permute-start.4 = (f32[256,512]{1,0:T(8,128)}, f32[256,512]{1,0:T(8,128)S(1)}, u32[]{:S(2)}, u32[]{:S(2)}) collective-permute-start(f32[256,512]{1,0:T(8,128)} %get-tuple-element.82), channel_id=1, source_target_pairs={{0,0},{1,4},{2,1},{3,5},{4,2},{5,6},{6,3},{7,7},{8,11},{9,15},{10,... | collective-permute-start | bytes 1572872 | tf_op jit(solution)/shard_map/ppermute | solution.py:153
  46.5 28.4 %collective-permute-start.5 = (f32[256,512]{1,0:T(8,128)}, f32[256,512]{1,0:T(8,128)}, u32[]{:S(2)}, u32[]{:S(2)}) collective-permute-start(f32[256,512]{1,0:T(8,128)} %get-tuple-element.81), channel_id=1, source_target_pairs={{0,0},{1,4},{2,1},{3,5},{4,2},{5,6},{6,3},{7,7},{8,11},{9,15},{10,... | collective-permute-start | bytes 1572872 | tf_op jit(solution)/shard_map/ppermute | solution.py:153
  54.6 24.2 %collective-permute-start.12 = (f32[256,512]{1,0:T(8,128)S(1)}, f32[256,512]{1,0:T(8,128)S(1)}, u32[]{:S(2)}, u32[]{:S(2)}) collective-permute-start(f32[256,512]{1,0:T(8,128)S(1)} %get-tuple-element.45.refs_0_.outer), channel_id=1, source_target_pairs={{4,1},{5,2},{6,3},{7,11},{15,10},{14,9},{13,8},{12,16},{20,17},{21... | collective-permute-start | bytes 1572872 | tf_op jit(solution)/shard_map/ppermute | solution.py:153
  55.5 23.4 %collective-permute-start.13 = (f32[256,512]{1,0:T(8,128)S(1)}, f32[256,512]{1,0:T(8,128)S(1)}, u32[]{:S(2)}, u32[]{:S(2)}) collective-permute-start(f32[256,512]{1,0:T(8,128)S(1)} %get-tuple-element.46.refs_1_.inner), channel_id=1, source_target_pairs={{0,4},{4,0},{1,5},{5,1},{2,6},{6,2},{3,7},{7,3},{11,15},{15,11},{1... | collective-permute-start | bytes 1572872 | tf_op jit(solution)/shard_map/ppermute | solution.py:153
  74.8 8.0 %collective-permute-start = (f32[256,512]{1,0:T(8,128)S(1)}, f32[256,512]{1,0:T(8,128)S(1)}, u32[]{:S(2)}, u32[]{:S(2)}) collective-permute-start(f32[256,512]{1,0:T(8,128)S(1)} %get-tuple-element.42), channel_id=1, source_target_pairs={{0,4},{1,5},{2,6},{3,7},{4,0},{5,1},{6,2},{7,3},{8,12},{9,13},{10,... | collective-permute-start | bytes 1572872 | tf_op jit(solution)/shard_map/ppermute | solution.py:153
  78.3 12.9 %collective-permute-start.11 = (f32[256,512]{1,0:T(8,128)S(1)}, f32[256,512]{1,0:T(8,128)S(1)}, u32[]{:S(2)}, u32[]{:S(2)}) collective-permute-start(f32[256,512]{1,0:T(8,128)S(1)} %get-tuple-element.48), channel_id=1, source_target_pairs={{0,4},{1,5},{2,6},{3,7},{4,0},{5,1},{6,2},{7,3},{8,12},{9,13},{10,... | collective-permute-start | bytes 1572872 | tf_op jit(solution)/shard_map/ppermute | solution.py:153
  81.9 9.4 %collective-permute-start.14 = (f32[256,512]{1,0:T(8,128)S(1)}, f32[256,512]{1,0:T(8,128)S(1)}, u32[]{:S(2)}, u32[]{:S(2)}) collective-permute-start(f32[256,512]{1,0:T(8,128)S(1)} %get-tuple-element.52), channel_id=1, source_target_pairs={{0,4},{1,5},{2,6},{3,7},{4,0},{5,1},{6,2},{7,3},{8,12},{9,13},{10,... | collective-permute-start | bytes 1572872 | tf_op jit(solution)/shard_map/ppermute | solution.py:153
  82.9 13.3 %collective-permute-start.21 = (f32[256,512]{1,0:T(8,128)S(1)}, f32[256,512]{1,0:T(8,128)S(1)}, u32[]{:S(2)}, u32[]{:S(2)}) collective-permute-start(f32[256,512]{1,0:T(8,128)S(1)} %get-tuple-element.49.refs_0_.outer), channel_id=1, source_target_pairs={{4,1},{5,2},{6,3},{7,11},{15,10},{14,9},{13,8},{12,16},{20,17},{21... | collective-permute-start | bytes 1572872 | tf_op jit(solution)/shard_map/ppermute | solution.py:153
  83.6 17.4 %collective-permute-start.22 = (f32[256,512]{1,0:T(8,128)S(1)}, f32[256,512]{1,0:T(8,128)S(1)}, u32[]{:S(2)}, u32[]{:S(2)}) collective-permute-start(f32[256,512]{1,0:T(8,128)S(1)} %get-tuple-element.50.refs_1_.inner), channel_id=1, source_target_pairs={{0,4},{4,0},{1,5},{5,1},{2,6},{6,2},{3,7},{7,3},{11,15},{15,11},{1... | collective-permute-start | bytes 1572872 | tf_op jit(solution)/shard_map/ppermute | solution.py:153
  91.5 22.7 %collective-permute-start.17 = (f32[2,64,512]{2,1,0:T(8,128)S(1)}, f32[2,64,512]{2,1,0:T(8,128)S(1)}, u32[]{:S(2)}, u32[]{:S(2)}) collective-permute-start(f32[2,64,512]{2,1,0:T(8,128)S(1)} %get-tuple-element.77), channel_id=1, source_target_pairs={{0,24},{1,25},{2,26},{3,27},{4,28},{5,29},{6,30},{7,31},{8,0},{9,1... | collective-permute-start | bytes 786440 | tf_op jit(solution)/shard_map/ppermute | solution.py:153
  95.5 9.5 %collective-permute-start.3 = (f32[1,64,512]{2,1,0:T(8,128)S(1)}, f32[1,64,512]{2,1,0:T(8,128)S(1)}, u32[]{:S(2)}, u32[]{:S(2)}) collective-permute-start(f32[1,64,512]{2,1,0:T(8,128)S(1)} %get-tuple-element.90), channel_id=1, source_target_pairs={{0,24},{1,25},{2,26},{3,27},{4,28},{5,29},{6,30},{7,31},{8,0},{9,1... | collective-permute-start | bytes 393224 | tf_op jit(solution)/shard_map/ppermute | solution.py:153
  95.6 17.9 %collective-permute-start.2 = (f32[1,64,512]{2,1,0:T(8,128)S(1)}, f32[1,64,512]{2,1,0:T(8,128)S(1)}, u32[]{:S(2)}, u32[]{:S(2)}) collective-permute-start(f32[1,64,512]{2,1,0:T(8,128)S(1)} %get-tuple-element.91), channel_id=1, source_target_pairs={{0,16},{1,17},{2,18},{3,19},{4,20},{5,21},{6,22},{7,23},{8,24},{9,... | collective-permute-start | bytes 393224 | tf_op jit(solution)/shard_map/ppermute | solution.py:153
  96.2 18.0 %collective-permute-start.1 = (f32[1,64,512]{2,1,0:T(8,128)S(1)}, f32[1,64,512]{2,1,0:T(8,128)S(1)}, u32[]{:S(2)}, u32[]{:S(2)}) collective-permute-start(f32[1,64,512]{2,1,0:T(8,128)S(1)} %get-tuple-element.89), channel_id=1, source_target_pairs={{0,8},{1,9},{2,10},{3,11},{4,12},{5,13},{6,14},{7,15},{8,16},{9,17... | collective-permute-start | bytes 393224 | tf_op jit(solution)/shard_map/ppermute | solution.py:153
  101.0 21.8 %collective-permute-start.16 = (f32[2,64,512]{2,1,0:T(8,128)S(1)}, f32[2,64,512]{2,1,0:T(8,128)S(1)}, u32[]{:S(2)}, u32[]{:S(2)}) collective-permute-start(f32[2,64,512]{2,1,0:T(8,128)S(1)} %get-tuple-element.78), channel_id=1, source_target_pairs={{0,16},{1,17},{2,18},{3,19},{4,20},{5,21},{6,22},{7,23},{8,24},{9,... | collective-permute-start | bytes 786440 | tf_op jit(solution)/shard_map/ppermute | solution.py:153
  105.0 17.8 %collective-permute-start.15 = (f32[2,64,512]{2,1,0:T(8,128)S(1)}, f32[2,64,512]{2,1,0:T(8,128)S(1)}, u32[]{:S(2)}, u32[]{:S(2)}) collective-permute-start(f32[2,64,512]{2,1,0:T(8,128)S(1)} %get-tuple-element.76), channel_id=1, source_target_pairs={{0,8},{1,9},{2,10},{3,11},{4,12},{5,13},{6,14},{7,15},{8,16},{9,17... | collective-permute-start | bytes 786440 | tf_op jit(solution)/shard_map/ppermute | solution.py:153
  113.5 10.8 %collective-permute-start.24 = (f32[256,512]{1,0:T(8,128)S(1)}, f32[256,512]{1,0:T(8,128)S(1)}, u32[]{:S(2)}, u32[]{:S(2)}) collective-permute-start(f32[256,512]{1,0:T(8,128)S(1)} %get-tuple-element.53.refs_0_.outer), channel_id=1, source_target_pairs={{4,1},{5,2},{6,3},{7,11},{15,10},{14,9},{13,8},{12,16},{20,17},{21... | collective-permute-start | bytes 1572872 | tf_op jit(solution)/shard_map/ppermute | solution.py:153
  114.2 10.1 %collective-permute-start.25 = (f32[256,512]{1,0:T(8,128)S(1)}, f32[256,512]{1,0:T(8,128)S(1)}, u32[]{:S(2)}, u32[]{:S(2)}) collective-permute-start(f32[256,512]{1,0:T(8,128)S(1)} %get-tuple-element.54.refs_1_.inner), channel_id=1, source_target_pairs={{0,4},{4,0},{1,5},{5,1},{2,6},{6,2},{3,7},{7,3},{11,15},{15,11},{1... | collective-permute-start | bytes 1572872 | tf_op jit(solution)/shard_map/ppermute | solution.py:153
  114.3 16.1 %collective-permute-start.23 = (f32[256,512]{1,0:T(8,128)S(1)}, f32[256,512]{1,0:T(8,128)S(1)}, u32[]{:S(2)}, u32[]{:S(2)}) collective-permute-start(f32[256,512]{1,0:T(8,128)S(1)} %get-tuple-element.56), channel_id=1, source_target_pairs={{0,4},{1,5},{2,6},{3,7},{4,0},{5,1},{6,2},{7,3},{8,12},{9,13},{10,... | collective-permute-start | bytes 1572872 | tf_op jit(solution)/shard_map/ppermute | solution.py:153
  122.9 10.5 %collective-permute-start.18 = (f32[3,64,512]{2,1,0:T(8,128)S(1)}, f32[3,64,512]{2,1,0:T(8,128)S(1)}, u32[]{:S(2)}, u32[]{:S(2)}) collective-permute-start(f32[3,64,512]{2,1,0:T(8,128)S(1)} %pad_maximum_fusion), channel_id=1, source_target_pairs={{0,1},{4,5},{8,9},{12,13},{16,17},{20,21},{24,25},{28,29},{3,2},{7... | collective-permute-start | bytes 1179656 | tf_op jit(solution)/shard_map/ppermute | solution.py:153
  126.4 9.3 %collective-permute-start.33 = (f32[256,512]{1,0:T(8,128)S(1)}, f32[256,512]{1,0:T(8,128)S(1)}, u32[]{:S(2)}, u32[]{:S(2)}) collective-permute-start(f32[256,512]{1,0:T(8,128)S(1)} %get-tuple-element.57.refs_0_.outer), channel_id=1, source_target_pairs={{4,1},{5,2},{6,3},{7,11},{15,10},{14,9},{13,8},{12,16},{20,17},{21... | collective-permute-start | bytes 1572872 | tf_op jit(solution)/shard_map/ppermute | solution.py:153
  127.1 8.6 %collective-permute-start.34 = (f32[256,512]{1,0:T(8,128)S(1)}, f32[256,512]{1,0:T(8,128)S(1)}, u32[]{:S(2)}, u32[]{:S(2)}) collective-permute-start(f32[256,512]{1,0:T(8,128)S(1)} %get-tuple-element.58.refs_1_.inner), channel_id=1, source_target_pairs={{0,4},{4,0},{1,5},{5,1},{2,6},{6,2},{3,7},{7,3},{11,15},{15,11},{1... | collective-permute-start | bytes 1572872 | tf_op jit(solution)/shard_map/ppermute | solution.py:153
  130.3 12.3 %collective-permute-start.26 = (f32[256,512]{1,0:T(8,128)S(1)}, f32[256,512]{1,0:T(8,128)S(1)}, u32[]{:S(2)}, u32[]{:S(2)}) collective-permute-start(f32[256,512]{1,0:T(8,128)S(1)} %get-tuple-element.60), channel_id=1, source_target_pairs={{0,4},{1,5},{2,6},{3,7},{4,0},{5,1},{6,2},{7,3},{8,12},{9,13},{10,... | collective-permute-start | bytes 1572872 | tf_op jit(solution)/shard_map/ppermute | solution.py:153
  134.3 14.0 %collective-permute-start.19 = (f32[3,64,512]{2,1,0:T(8,128)}, f32[3,64,512]{2,1,0:T(8,128)}, u32[]{:S(2)}, u32[]{:S(2)}) collective-permute-start(f32[3,64,512]{2,1,0:T(8,128)} %fusion.18), channel_id=1, source_target_pairs={{1,2},{5,6},{9,10},{13,14},{17,18},{21,22},{25,26},{29,30},{2,1},{... | collective-permute-start | bytes 1179656 | tf_op jit(solution)/shard_map/ppermute | solution.py:153
  138.7 31.9 %collective-permute-start.35 = (f32[256,512]{1,0:T(8,128)S(1)}, f32[256,512]{1,0:T(8,128)}, u32[]{:S(2)}, u32[]{:S(2)}) collective-permute-start(f32[256,512]{1,0:T(8,128)S(1)} %get-tuple-element.64), channel_id=1, source_target_pairs={{0,4},{1,5},{2,6},{3,7},{4,0},{5,1},{6,2},{7,3},{8,12},{9,13},{10,... | collective-permute-start | bytes 1572872 | tf_op jit(solution)/shard_map/ppermute | solution.py:153
  143.8 9.5 %collective-permute-start.29 = (f32[2,64,512]{2,1,0:T(8,128)}, f32[2,64,512]{2,1,0:T(8,128)}, u32[]{:S(2)}, u32[]{:S(2)}) collective-permute-start(f32[2,64,512]{2,1,0:T(8,128)} %get-tuple-element.74), channel_id=1, source_target_pairs={{0,24},{1,25},{2,26},{3,27},{4,28},{5,29},{6,30},{7,31},{8,0},{9,1... | collective-permute-start | bytes 786440 | tf_op jit(solution)/shard_map/ppermute | solution.py:153
  143.8 19.8 %collective-permute-start.28 = (f32[2,64,512]{2,1,0:T(8,128)}, f32[2,64,512]{2,1,0:T(8,128)}, u32[]{:S(2)}, u32[]{:S(2)}) collective-permute-start(f32[2,64,512]{2,1,0:T(8,128)} %get-tuple-element.75), channel_id=1, source_target_pairs={{0,16},{1,17},{2,18},{3,19},{4,20},{5,21},{6,22},{7,23},{8,24},{9,... | collective-permute-start | bytes 786440 | tf_op jit(solution)/shard_map/ppermute | solution.py:153
  146.2 18.6 %collective-permute-start.27 = (f32[2,64,512]{2,1,0:T(8,128)}, f32[2,64,512]{2,1,0:T(8,128)}, u32[]{:S(2)}, u32[]{:S(2)}) collective-permute-start(f32[2,64,512]{2,1,0:T(8,128)} %get-tuple-element.73), channel_id=1, source_target_pairs={{0,8},{1,9},{2,10},{3,11},{4,12},{5,13},{6,14},{7,15},{8,16},{9,17... | collective-permute-start | bytes 786440 | tf_op jit(solution)/shard_map/ppermute | solution.py:153
  148.3 23.6 %collective-permute-start.42 = (f32[256,512]{1,0:T(8,128)S(1)}, f32[256,512]{1,0:T(8,128)S(1)}, u32[]{:S(2)}, u32[]{:S(2)}) collective-permute-start(f32[256,512]{1,0:T(8,128)S(1)} %get-tuple-element.61.refs_0_.outer), channel_id=1, source_target_pairs={{4,1},{5,2},{6,3},{7,11},{15,10},{14,9},{13,8},{12,16},{20,17},{21... | collective-permute-start | bytes 1572872 | tf_op jit(solution)/shard_map/ppermute | solution.py:153
  153.3 21.2 %collective-permute-start.43 = (f32[256,512]{1,0:T(8,128)S(1)}, f32[256,512]{1,0:T(8,128)S(1)}, u32[]{:S(2)}, u32[]{:S(2)}) collective-permute-start(f32[256,512]{1,0:T(8,128)S(1)} %get-tuple-element.62.refs_1_.inner), channel_id=1, source_target_pairs={{0,4},{4,0},{1,5},{5,1},{2,6},{6,2},{3,7},{7,3},{11,15},{15,11},{1... | collective-permute-start | bytes 1572872 | tf_op jit(solution)/shard_map/ppermute | solution.py:153
  163.6 19.4 %collective-permute-start.20 = (f32[3,64,512]{2,1,0:T(8,128)S(1)}, f32[3,64,512]{2,1,0:T(8,128)S(1)}, u32[]{:S(2)}, u32[]{:S(2)}) collective-permute-start(f32[3,64,512]{2,1,0:T(8,128)S(1)} %add.135), channel_id=1, source_target_pairs={{1,0},{5,4},{9,8},{13,12},{17,16},{21,20},{25,24},{29,28}} | collective-permute-start | bytes 1179656 | tf_op jit(solution)/shard_map/ppermute | solution.py:153
  166.1 13.4 %collective-permute-start.30 = (f32[2,64,512]{2,1,0:T(8,128)S(1)}, f32[2,64,512]{2,1,0:T(8,128)S(1)}, u32[]{:S(2)}, u32[]{:S(2)}) collective-permute-start(f32[2,64,512]{2,1,0:T(8,128)S(1)} %fusion.4), channel_id=1, source_target_pairs={{0,1},{4,5},{8,9},{12,13},{16,17},{20,21},{24,25},{28,29},{3,2},{7... | collective-permute-start | bytes 786440 | tf_op jit(solution)/shard_map/ppermute | solution.py:153
  171.8 7.8 %collective-permute-start.38 = (f32[1,64,512]{2,1,0:T(8,128)S(1)}, f32[1,64,512]{2,1,0:T(8,128)S(1)}, u32[]{:S(2)}, u32[]{:S(2)}) collective-permute-start(f32[1,64,512]{2,1,0:T(8,128)S(1)} %get-tuple-element.87), channel_id=1, source_target_pairs={{0,24},{1,25},{2,26},{3,27},{4,28},{5,29},{6,30},{7,31},{8,0},{9,1... | collective-permute-start | bytes 393224 | tf_op jit(solution)/shard_map/ppermute | solution.py:153
  171.9 8.4 %collective-permute-start.37 = (f32[1,64,512]{2,1,0:T(8,128)S(1)}, f32[1,64,512]{2,1,0:T(8,128)S(1)}, u32[]{:S(2)}, u32[]{:S(2)}) collective-permute-start(f32[1,64,512]{2,1,0:T(8,128)S(1)} %get-tuple-element.88), channel_id=1, source_target_pairs={{0,16},{1,17},{2,18},{3,19},{4,20},{5,21},{6,22},{7,23},{8,24},{9,... | collective-permute-start | bytes 393224 | tf_op jit(solution)/shard_map/ppermute | solution.py:153
  179.5 9.6 %collective-permute-start.44 = (f32[256,512]{1,0:T(8,128)S(1)}, f32[256,512]{1,0:T(8,128)S(1)}, u32[]{:S(2)}, u32[]{:S(2)}) collective-permute-start(f32[256,512]{1,0:T(8,128)S(1)} %get-tuple-element.68), channel_id=1, source_target_pairs={{0,4},{1,5},{2,6},{3,7},{4,0},{5,1},{6,2},{7,3},{8,12},{9,13},{10,... | collective-permute-start | bytes 1572872 | tf_op jit(solution)/shard_map/ppermute | solution.py:153
  179.6 7.4 %collective-permute-start.31 = (f32[2,64,512]{2,1,0:T(8,128)S(1)}, f32[2,64,512]{2,1,0:T(8,128)S(1)}, u32[]{:S(2)}, u32[]{:S(2)}) collective-permute-start(f32[2,64,512]{2,1,0:T(8,128)S(1)} %add.141), channel_id=1, source_target_pairs={{1,2},{5,6},{9,10},{13,14},{17,18},{21,22},{25,26},{29,30},{2,1},{... | collective-permute-start | bytes 786440 | tf_op jit(solution)/shard_map/ppermute | solution.py:153
  187.1 12.3 %collective-permute-start.32 = (f32[2,64,512]{2,1,0:T(8,128)S(1)}, f32[2,64,512]{2,1,0:T(8,128)S(1)}, u32[]{:S(2)}, u32[]{:S(2)}) collective-permute-start(f32[2,64,512]{2,1,0:T(8,128)S(1)} %add.142), channel_id=1, source_target_pairs={{1,0},{5,4},{9,8},{13,12},{17,16},{21,20},{25,24},{29,28},{2,3},{6... | collective-permute-start | bytes 786440 | tf_op jit(solution)/shard_map/ppermute | solution.py:153
  189.2 10.2 %collective-permute-start.47 = (f32[1,64,512]{2,1,0:T(8,128)S(1)}, f32[1,64,512]{2,1,0:T(8,128)S(1)}, u32[]{:S(2)}, u32[]{:S(2)}) collective-permute-start(f32[1,64,512]{2,1,0:T(8,128)S(1)} %get-tuple-element.84), channel_id=1, source_target_pairs={{0,24},{1,25},{2,26},{3,27},{4,28},{5,29},{6,30},{7,31},{8,0},{9,1... | collective-permute-start | bytes 393224 | tf_op jit(solution)/shard_map/ppermute | solution.py:153
  190.3 9.1 %collective-permute-start.46 = (f32[1,64,512]{2,1,0:T(8,128)S(1)}, f32[1,64,512]{2,1,0:T(8,128)S(1)}, u32[]{:S(2)}, u32[]{:S(2)}) collective-permute-start(f32[1,64,512]{2,1,0:T(8,128)S(1)} %get-tuple-element.85), channel_id=1, source_target_pairs={{0,16},{1,17},{2,18},{3,19},{4,20},{5,21},{6,22},{7,23},{8,24},{9,... | collective-permute-start | bytes 393224 | tf_op jit(solution)/shard_map/ppermute | solution.py:153
  190.8 8.7 %collective-permute-start.45 = (f32[1,64,512]{2,1,0:T(8,128)S(1)}, f32[1,64,512]{2,1,0:T(8,128)S(1)}, u32[]{:S(2)}, u32[]{:S(2)}) collective-permute-start(f32[1,64,512]{2,1,0:T(8,128)S(1)} %get-tuple-element.83), channel_id=1, source_target_pairs={{0,8},{1,9},{2,10},{3,11},{4,12},{5,13},{6,14},{7,15},{8,16},{9,17... | collective-permute-start | bytes 393224 | tf_op jit(solution)/shard_map/ppermute | solution.py:153
  199.5 8.0 %collective-permute-start.50 = (f32[1,64,512]{2,1,0:T(8,128)S(1)}, f32[1,64,512]{2,1,0:T(8,128)S(1)}, u32[]{:S(2)}, u32[]{:S(2)}) collective-permute-start(f32[1,64,512]{2,1,0:T(8,128)S(1)} %fusion.13), channel_id=1, source_target_pairs={{2,3},{6,7},{10,11},{14,15},{18,19},{22,23},{26,27},{30,31}} | collective-permute-start | bytes 393224 | tf_op jit(solution)/shard_map/ppermute | solution.py:153
  200.2 7.3 %collective-permute-start.49 = (f32[1,64,512]{2,1,0:T(8,128)S(1)}, f32[1,64,512]{2,1,0:T(8,128)S(1)}, u32[]{:S(2)}, u32[]{:S(2)}) collective-permute-start(f32[1,64,512]{2,1,0:T(8,128)S(1)} %fusion.13), channel_id=1, source_target_pairs={{1,3},{5,7},{9,11},{13,15},{17,19},{21,23},{25,27},{29,31}} | collective-permute-start | bytes 393224 | tf_op jit(solution)/shard_map/ppermute | solution.py:153
  200.8 9.1 %collective-permute-start.48 = (f32[1,64,512]{2,1,0:T(8,128)S(1)}, f32[1,64,512]{2,1,0:T(8,128)S(1)}, u32[]{:S(2)}, u32[]{:S(2)}) collective-permute-start(f32[1,64,512]{2,1,0:T(8,128)S(1)} %fusion.13), channel_id=1, source_target_pairs={{0,3},{4,7},{8,11},{12,15},{16,19},{20,23},{24,27},{28,31}} | collective-permute-start | bytes 393224 | tf_op jit(solution)/shard_map/ppermute | solution.py:153
  210.7 6.0 %collective-permute-start.51 = (f32[64,512]{1,0:T(8,128)S(1)}, f32[64,512]{1,0:T(8,128)S(1)}, u32[]{:S(2)}, u32[]{:S(2)}) collective-permute-start(f32[64,512]{1,0:T(8,128)S(1)} %get-tuple-element.70), channel_id=1, source_target_pairs={{0,8},{1,9},{2,10},{3,11},{4,12},{5,13},{6,14},{7,15},{8,16},{9,17... | collective-permute-start | bytes 393224 | tf_op jit(solution)/shard_map/ppermute | solution.py:153
  210.8 6.4 %collective-permute-start.52 = (f32[64,512]{1,0:T(8,128)S(1)}, f32[64,512]{1,0:T(8,128)S(1)}, u32[]{:S(2)}, u32[]{:S(2)}) collective-permute-start(f32[64,512]{1,0:T(8,128)S(1)} %get-tuple-element.71), channel_id=1, source_target_pairs={{0,16},{1,17},{2,18},{3,19},{4,20},{5,21},{6,22},{7,23},{8,24},{9,... | collective-permute-start | bytes 393224 | tf_op jit(solution)/shard_map/ppermute | solution.py:153
  (17 other events, 252.0 us)
